TPU v7x, 32 devices: a whole 2x2x4 slice. The times are simulated.
32 devices in a mesh: space: 16 (over z, x, core), vel: 2 (over y).
Axes of the slice: x: 2, y: 2, z: 4, core: 2. Of those that a mesh axis runs over, the one named last changes fastest.
Arguments:
- dist: float32 [64, 8, 8, 4096], P('space', None, None, 'vel'), may hold values from 0 to 5.5, as said below
- cell_type: int32 [64, 8, 8], replicated, may hold values from 0 to 3, as said below
- boundary: float32 [6], replicated, may hold values from 0.8 to 1.2
Outputs:
- renewed: float32 [64, 8, 8, 4096], P('space', None, None, 'vel')
Inputs may be any that keep to these rules, and one draw needn't show every extreme that they name: `dist`: every entry is positive. `cell_type`: cells of kind 1 never lie on the grid's outer layer; kind 2 lies only in the plane x = 0 and kind 3 only in the plane x = 63, and both occur in every draw.
All inputs are finite; a program needn't handle non-finite values.
Results may differ from a plain program's by a relative error of at most 0.0003.
Values sent between devices are 32-bit elements; how exact they have to be, the bound alone decides.
No kernel may reach another device: no remote copies, remote signals or barrier semaphores. Data moves between devices by JAX's collectives and lax.ppermute only.
A program may use at most 64 MiB of HBM per device.

v0:
```python
import functools
import math

import jax
import jax.numpy as jnp
import numpy as np
from jax import lax
from jax.experimental import pallas as pl
from jax.experimental.pallas import tpu as pltpu
from jax.sharding import PartitionSpec as P

NODES = 16
STEPS = 2
PRANDTL = 2.0 / 3.0
OMEGA = 0.81
MU_REF = 0.1
DT = 0.1
HALF = 0.05
VMAX = 5.0
SPACING = 2.0 * VMAX / NODES
UNIT = 0.5 * SPACING
WEIGHT = SPACING**3 / (2.0 * math.pi) ** 1.5
LOG2E = 1.4426950408889634
COLS = 16
TILE = NODES * NODES
ROWS = 8
HALFTILE = 128


def node_table():
    number = np.arange(NODES**3)
    digits = (number // (NODES * NODES), number // NODES % NODES, number % NODES)
    m = [2 * d + 1 - NODES for d in digits]
    n = m[0] * m[0] + m[1] * m[1] + m[2] * m[2]
    third = [c * n for c in m]
    high = [((v + 32) // 64) * 64 for v in third]
    low = [v - h for v, h in zip(third, high)]
    base = [np.ones_like(n), *m, m[0] * m[0], m[1] * m[1], m[2] * m[2]]
    base += [m[0] * m[1], m[0] * m[2], m[1] * m[2], *high, *low]
    table = np.zeros((HALFTILE, NODES**3), np.float32)
    for part in range(3):
        table[part * COLS : (part + 1) * COLS] = np.stack(base)
    return jnp.asarray(table, jnp.bfloat16)


def dot_nt(a, b):
    return lax.dot_general(a, b, (((1,), (1,)), ((), ())), preferred_element_type=jnp.float32)


def dot_nn(a, b):
    return lax.dot_general(a, b, (((1,), (0,)), ((), ())), preferred_element_type=jnp.float32)


def split(value):
    high = value.astype(jnp.bfloat16)
    low = (value - high.astype(jnp.float32)).astype(jnp.bfloat16)
    return high, low


def state_of(t):
    density = t[0]
    second_unit = UNIT * UNIT
    velocity = [UNIT * t[1 + e] / density for e in range(3)]
    second = (
        (second_unit * t[4], second_unit * t[7], second_unit * t[8]),
        (second_unit * t[7], second_unit * t[5], second_unit * t[9]),
        (second_unit * t[8], second_unit * t[9], second_unit * t[6]),
    )
    trace = second[0][0] + second[1][1] + second[2][2]
    speed_sq = velocity[0] * velocity[0] + velocity[1] * velocity[1] + velocity[2] * velocity[2]
    temper = (trace / density - speed_sq) / 3.0
    heat = [
        0.5
        * (
            (UNIT**3) * (t[10 + e] + t[13 + e])
            - 2.0
            * (
                second[e][0] * velocity[0]
                + second[e][1] * velocity[1]
                + second[e][2] * velocity[2]
            )
            - velocity[e] * trace
            + 2.0 * density * velocity[e] * speed_sq
        )
        for e in range(3)
    ]
    return density, velocity, temper, heat


def relaxation(density, temper):
    return MU_REF * jnp.exp(OMEGA * jnp.log(temper)) / (density * temper)


def exponent_coefs(velocity, temper):
    g = -0.5 * LOG2E / temper
    speed_sq = velocity[0] * velocity[0] + velocity[1] * velocity[1] + velocity[2] * velocity[2]
    square = g * (UNIT * UNIT)
    zero = jnp.zeros_like(g)
    linear = [(-2.0 * UNIT) * g * velocity[e] for e in range(3)]
    return [g * speed_sq, *linear, square, square, square] + [zero] * 9


def shakhov_coefs(amplitude, density, velocity, temper, heat):
    factor = (1.0 - PRANDTL) / (5.0 * density * temper * temper)
    af = amplitude * factor
    inverse = 1.0 / temper
    along = velocity[0] * heat[0] + velocity[1] * heat[1] + velocity[2] * heat[2]
    speed_sq = velocity[0] * velocity[0] + velocity[1] * velocity[1] + velocity[2] * velocity[2]
    a2 = (UNIT * UNIT) * inverse
    b = [(-2.0 * UNIT) * velocity[e] * inverse for e in range(3)]
    c = speed_sq * inverse - 5.0
    kq = [UNIT * heat[e] for e in range(3)]
    cubic = [af * (kq[e] * a2) for e in range(3)]
    return [
        amplitude - af * (along * c),
        *[af * (kq[e] * c - along * b[e]) for e in range(3)],
        *[af * (kq[e] * b[e] - along * a2) for e in range(3)],
        af * (kq[0] * b[1] + kq[1] * b[0]),
        af * (kq[0] * b[2] + kq[2] * b[0]),
        af * (kq[1] * b[2] + kq[2] * b[1]),
        *cubic,
        *cubic,
    ]


def transposed_parts(coefs, extra, work):
    count = work.shape[1]
    work[...] = jnp.zeros(work.shape, jnp.float32)
    for row, value in enumerate(coefs):
        high = value.astype(jnp.bfloat16).astype(jnp.float32)
        rest = value - high
        middle = rest.astype(jnp.bfloat16).astype(jnp.float32)
        work[row : row + 1, :] = high
        work[COLS + row : COLS + row + 1, :] = middle
        work[2 * COLS + row : 2 * COLS + row + 1, :] = rest - middle
    if extra is not None:
        work[3 * COLS : 3 * COLS + 1, :] = extra
    return jnp.transpose(work[...], (1, 0))


def spread_column(matrix):
    return jnp.broadcast_to(matrix[:, 3 * COLS : 3 * COLS + 1], (matrix.shape[0], HALFTILE))


def twice(value):
    return jnp.concatenate([value, value], axis=1)


def lane_speeds(shape):
    lane = lax.broadcasted_iota(jnp.int32, shape, 1)
    along_y = (2 * (lane // NODES) + 1 - NODES).astype(jnp.float32) * UNIT
    along_z = (2 * (lane % NODES) + 1 - NODES).astype(jnp.float32) * UNIT
    return along_y, along_z


def moments_kernel(x_ref, table_ref, out_ref, acc_ref):
    n = pl.program_id(0)

    @pl.when(n == 0)
    def _():
        acc_ref[...] = jnp.zeros_like(acc_ref)

    high, low = split(x_ref[...])
    acc_ref[...] += dot_nt(high, table_ref[...]) + dot_nt(low, table_ref[...])

    @pl.when(n == pl.num_programs(0) - 1)
    def _():
        out_ref[...] = WEIGHT * jnp.transpose(acc_ref[...], (1, 0))[:COLS]


def faces_kernel(
    scal_ref, x_ref, upw_ref, dn_ref, tot_ref, mask_ref, table_ref,
    base_ref, face_ref, mom_ref,
    work_ref, full_ref, lhs_ref, alpha_ref, res_ref, slab_ref, high_ref, low_ref, acc_ref,
    *, planes,
):
    n = pl.program_id(0)
    neg = scal_ref[0]
    cells = ROWS * ROWS
    slots = planes + 3
    slab_rows = slots * cells
    inner = (ROWS - 2) * ROWS
    face_y = (planes + 1) * inner
    face_z = face_y + planes * cells
    faces = face_z + planes * inner

    @pl.when(n == 0)
    def _():
        t = [tot_ref[i : i + 1, :] for i in range(COLS)]
        density, velocity, temper, heat = state_of(t)
        tau = relaxation(density, temper)
        heat = [q / (1.0 + DT * PRANDTL / (2.0 * tau)) for q in heat]
        divide = 1.0 / (2.0 * tau + DT)
        alpha = (2.0 * tau - HALF) * divide
        beta = (3.0 * HALF) * divide
        amplitude = beta * (density / (temper * jnp.sqrt(temper)))
        turned = transposed_parts(exponent_coefs(velocity, temper), alpha, work_ref)
        full_ref[...] = turned
        first = pl.multiple_of(neg * cells, cells)
        part = full_ref[pl.ds(first, slab_rows), :]
        lhs_ref[0:slab_rows, :] = part.astype(jnp.bfloat16)
        alpha_ref[...] = spread_column(part)
        turned = transposed_parts(
            shakhov_coefs(amplitude, density, velocity, temper, heat), None, work_ref
        )
        full_ref[...] = turned
        part = full_ref[pl.ds(first, slab_rows), :]
        lhs_ref[slab_rows : 2 * slab_rows, :] = part.astype(jnp.bfloat16)
        acc_ref[...] = jnp.zeros_like(acc_ref)

    table = table_ref[...]
    res_ref[...] = dot_nn(lhs_ref[...], table)

    def before_of(src_ref, row, slot, base_row=None):
        for r in range(0, cells, 16):
            f = src_ref[row + r : row + r + 16, :]
            at = pl.multiple_of(slot * cells + r, 16)
            exponent = res_ref[pl.ds(at, 16), :]
            poly = res_ref[pl.ds(pl.multiple_of(at + slab_rows, 16), 16), :]
            b = twice(alpha_ref[pl.ds(at, 16), :]) * f + jnp.exp2(exponent) * poly
            slab_ref[slot, r : r + 16, :] = b
            if base_row is not None:
                base_ref[base_row + r : base_row + r + 16, :] = (4.0 / 3.0) * b - (1.0 / 3.0) * f

    for p in range(planes):
        before_of(x_ref, p * cells, p + 2 - neg, p * cells)
    before_of(upw_ref, 0, (planes + 1) * neg)
    before_of(upw_ref, cells, (planes + 1) * neg + 1)
    before_of(dn_ref, 0, (planes + 2) * (1 - neg))

    along_y, along_z = lane_speeds((ROWS, TILE))
    lane = lax.broadcasted_iota(jnp.int32, (ROWS, TILE), 1)
    z_minus = (lane % NODES) < NODES // 2
    ky = HALF * along_y
    kz = HALF * along_z
    hy = jnp.where(lane < HALFTILE, -0.5, 0.5)
    hz = jnp.where(z_minus, -0.5, 0.5)
    digit = scal_ref[1] + n
    along_x = (2 * digit + 1 - NODES).astype(jnp.float32) * UNIT
    kx = HALF * along_x
    hx = jnp.where(along_x > 0, 0.5, -0.5)

    def middle(a, b):
        return jnp.maximum(jnp.minimum(a, b), jnp.minimum(jnp.maximum(a, b), 0.0))

    def put(row, pair):
        both = jnp.concatenate(pair, axis=0)
        high, low = split(both)
        at = pl.ds(pl.multiple_of(row, 16), 16)
        face_ref[at, :] = both
        high_ref[at, :] = high
        low_ref[at, :] = low

    def plane_faces(slot, own):
        def col(y):
            return slab_ref[slot, y * ROWS : (y + 1) * ROWS, :]

        values = {0: col(0), 1: col(1)}
        diff = values[1] - values[0]
        fx, fy, fz = {}, {0: values[0], ROWS - 1: col(ROWS - 1)}, {}
        for y in range(1, ROWS - 1):
            here = values[y]
            values[y + 1] = col(y + 1)
            back, diff = diff, values[y + 1] - here
            rows = slice(y * ROWS, (y + 1) * ROWS)
            mask = twice(mask_ref[pl.ds(pl.multiple_of(slot * cells + y * ROWS, ROWS), ROWS), :])
            slope_y = middle(diff, back) * mask
            slope_x = mask * middle(
                slab_ref[slot + 1, rows, :] - here, here - slab_ref[slot - 1, rows, :]
            )
            step = here - pltpu.roll(here, 1, 0)
            slope_z = middle(pltpu.roll(step, ROWS - 1, 0), step) * mask
            centre = here - (kx * slope_x + ky * slope_y + kz * slope_z)
            fx[y] = centre + hx * slope_x
            if own is not None:
                fy[y] = centre + hy * slope_y
                side = centre + hz * slope_z
                fz[y] = jnp.where(z_minus, side, pltpu.roll(side, 1, 0))
        for i in range((ROWS - 2) // 2):
            row = (slot - 1) * inner + 16 * i
            put(row, [fx[1 + 2 * i], fx[2 + 2 * i]])
        if own is not None:
            gy = [fy[0]]
            for j in range(1, ROWS):
                gy.append(jnp.concatenate([fy[j][:, :HALFTILE], fy[j - 1][:, HALFTILE:]], axis=1))
            for i in range(ROWS // 2):
                put(face_y + own * cells + 16 * i, [gy[2 * i], gy[2 * i + 1]])
            for i in range((ROWS - 2) // 2):
                put(face_z + own * inner + 16 * i, [fz[1 + 2 * i], fz[2 + 2 * i]])

    for slot in range(2, planes + 1):
        plane_faces(slot, slot - 2 + neg)
    edge = (planes + 1) - planes * neg
    plane_faces(edge, edge - 2 + neg)
    plane_faces(1 + planes * neg, None)

    acc_ref[0:faces, :] += dot_nt(high_ref[...], table) + dot_nt(low_ref[...], table)

    @pl.when(n == pl.num_programs(0) - 1)
    def _():
        mom_ref[...] = WEIGHT * jnp.transpose(acc_ref[...], (1, 0))[:COLS]


def renew_kernel(
    scal_ref, bound_ref, base_ref, face_ref, mom_ref, tot_ref, kind_ref, mask_ref, table_ref,
    out_ref,
    work_ref, wide_ref, lhs_ref, keep_ref, amp_ref, res_ref, flux_ref,
    *, planes,
):
    n = pl.program_id(0)
    cells = ROWS * ROWS
    inner = (ROWS - 2) * ROWS
    face_y = (planes + 1) * inner
    face_z = face_y + planes * cells
    faces = face_z + planes * inner
    own = planes * cells

    @pl.when(n == 0)
    def _():
        t = [mom_ref[i : i + 1, :] for i in range(COLS)]
        density, velocity, temper, heat = state_of(t)
        tau = relaxation(density, temper)
        heat = [2.0 * tau * q / (2.0 * tau + HALF * PRANDTL) for q in heat]
        divide = 1.0 / (2.0 * tau + HALF)
        keep = 2.0 * tau * divide
        amplitude = (HALF * divide) * (density / (temper * jnp.sqrt(temper)))
        turned = transposed_parts(exponent_coefs(velocity, temper), keep, wide_ref)[:faces]
        lhs_ref[0:faces, :] = turned.astype(jnp.bfloat16)
        keep_ref[...] = spread_column(turned)
        turned = transposed_parts(
            shakhov_coefs(amplitude, density, velocity, temper, heat), None, wide_ref
        )[:faces]
        lhs_ref[faces : 2 * faces, :] = turned.astype(jnp.bfloat16)

        density = tot_ref[0:1, :]
        kind = kind_ref[...]
        inlet, outlet = kind == 2, kind == 3
        moving = [
            jnp.where(outlet, UNIT * tot_ref[1 + e : 2 + e, :] / density, 0.0) for e in range(3)
        ]
        moving[0] = jnp.where(inlet, bound_ref[1], moving[0])
        dense = jnp.where(inlet, bound_ref[0], jnp.where(outlet, bound_ref[3], density))
        warm = jnp.where(inlet, bound_ref[2], jnp.where(outlet, bound_ref[4], bound_ref[5]))
        amplitude = dense / (warm * jnp.sqrt(warm))
        turned = transposed_parts(exponent_coefs(moving, warm), amplitude, work_ref)
        lhs_ref[2 * faces : 2 * faces + own, :] = turned.astype(jnp.bfloat16)
        amp_ref[...] = spread_column(turned)

    res_ref[...] = dot_nn(lhs_ref[...], table_ref[...])

    for r in range(0, faces, 16):
        rows = slice(r, r + 16)
        poly = res_ref[faces + r : faces + r + 16, :]
        flux_ref[rows, :] = (
            twice(keep_ref[rows, :]) * face_ref[rows, :] + jnp.exp2(res_ref[rows, :]) * poly
        )

    along_y, along_z = lane_speeds((ROWS, TILE))
    hy = DT * along_y
    hz = DT * along_z
    digit = scal_ref[1] + n
    hx = (2 * digit + 1 - NODES).astype(jnp.float32) * (UNIT * DT)

    for p in range(planes):
        for y in range(ROWS):
            at = p * cells + y * ROWS
            rows = slice(at, at + ROWS)
            other = twice(amp_ref[rows, :]) * jnp.exp2(
                res_ref[2 * faces + at : 2 * faces + at + ROWS, :]
            )
            if 0 < y < ROWS - 1:
                ax = p * inner + (y - 1) * ROWS
                ay = face_y + at
                az = face_z + ax
                along = flux_ref[ax + inner : ax + inner + ROWS, :] - flux_ref[ax : ax + ROWS, :]
                across = flux_ref[ay + ROWS : ay + 2 * ROWS, :] - flux_ref[ay : ay + ROWS, :]
                low = flux_ref[az : az + ROWS, :]
                rise = pltpu.roll(low, ROWS - 1, 0) - low
                fresh = base_ref[rows, :] - (hx * along + hy * across + hz * rise)
                out_ref[rows, :] = jnp.where(twice(mask_ref[rows, :]) > 0.0, fresh, other)
            else:
                out_ref[rows, :] = other


def on_device(dist, cell_type, boundary, *, spaces, vels):
    planes, across, height, local = dist.shape
    cells = across * height
    own = planes * cells
    inner = cells - 2 * height
    faces = (planes + 1) * inner + planes * cells + planes * inner
    padded = -(-faces // 128) * 128
    slots = planes + 3
    slab_rows = slots * cells
    steps = local // TILE
    space, vel = lax.axis_index("space"), lax.axis_index("vel")
    neg = (vel < vels // 2).astype(jnp.int32)
    scal = jnp.stack([neg, vel * steps]).astype(jnp.int32)
    table = lax.dynamic_slice_in_dim(node_table(), vel * local, local, 1)

    kinds = jnp.pad(cell_type, ((2, 2), (0, 0), (0, 0)))
    kinds = lax.dynamic_slice_in_dim(kinds, space * planes, planes + 4, 0).reshape(-1)
    fluid = jnp.broadcast_to((kinds == 1).astype(jnp.float32)[:, None], (kinds.size, HALFTILE))
    mask_slab = lax.dynamic_slice_in_dim(fluid, neg * cells, slab_rows, 0)
    mask_own = fluid[2 * cells : 2 * cells + own]
    kind_own = kinds[2 * cells : 2 * cells + own].reshape(1, own)

    whole = lambda *shape: pl.BlockSpec(shape, lambda n: (0,) * len(shape))
    tiled = lambda rows: pl.BlockSpec((rows, TILE), lambda n: (0, n))
    smem = pl.BlockSpec(memory_space=pltpu.SMEM)
    f32, bf16 = jnp.float32, jnp.bfloat16
    params = pltpu.CompilerParams(dimension_semantics=("arbitrary",))

    moments = pl.pallas_call(
        moments_kernel,
        grid=(steps,),
        in_specs=[tiled(own), tiled(HALFTILE)],
        out_specs=whole(COLS, own),
        out_shape=jax.ShapeDtypeStruct((COLS, own), f32),
        scratch_shapes=[pltpu.VMEM((own, HALFTILE), f32)],
        compiler_params=params,
        name="moments",
    )
    faces_call = pl.pallas_call(
        functools.partial(faces_kernel, planes=planes),
        grid=(steps,),
        in_specs=[
            smem, tiled(own), tiled(2 * cells), tiled(cells), whole(COLS, own + 4 * cells),
            whole(slab_rows, HALFTILE), tiled(HALFTILE),
        ],
        out_specs=[tiled(own), tiled(faces), whole(COLS, padded)],
        out_shape=[
            jax.ShapeDtypeStruct((own, local), f32),
            jax.ShapeDtypeStruct((faces, local), f32),
            jax.ShapeDtypeStruct((COLS, padded), f32),
        ],
        scratch_shapes=[
            pltpu.VMEM((HALFTILE, own + 4 * cells), f32),
            pltpu.VMEM((own + 4 * cells, HALFTILE), f32),
            pltpu.VMEM((2 * slab_rows, HALFTILE), bf16),
            pltpu.VMEM((slab_rows, HALFTILE), f32),
            pltpu.VMEM((2 * slab_rows, TILE), f32),
            pltpu.VMEM((slots, cells, TILE), f32),
            pltpu.VMEM((faces, TILE), bf16),
            pltpu.VMEM((faces, TILE), bf16),
            pltpu.VMEM((padded, HALFTILE), f32),
        ],
        compiler_params=params,
        name="faces",
    )
    renew = pl.pallas_call(
        functools.partial(renew_kernel, planes=planes),
        grid=(steps,),
        in_specs=[
            smem, smem, tiled(own), tiled(faces), whole(COLS, padded), whole(COLS, own),
            whole(1, own), whole(own, HALFTILE), tiled(HALFTILE),
        ],
        out_specs=tiled(own),
        out_shape=jax.ShapeDtypeStruct((own, local), f32),
        scratch_shapes=[
            pltpu.VMEM((HALFTILE, own), f32),
            pltpu.VMEM((HALFTILE, padded), f32),
            pltpu.VMEM((2 * faces + own, HALFTILE), bf16),
            pltpu.VMEM((faces, HALFTILE), f32),
            pltpu.VMEM((own, HALFTILE), f32),
            pltpu.VMEM((2 * faces + own, TILE), f32),
            pltpu.VMEM((faces, TILE), f32),
        ],
        compiler_params=params,
        name="renew",
    )

    upwind, downwind = [], []
    for s in range(spaces - 1):
        for v in range(vels):
            ahead = (s * vels + v, (s + 1) * vels + v)
            back = (ahead[1], ahead[0])
            upwind.append(back if v < vels // 2 else ahead)
            downwind.append(ahead if v < vels // 2 else back)
    rising = [(s, s + 1) for s in range(spaces - 1)]
    falling = [(s + 1, s) for s in range(spaces - 1)]

    def summed(part):
        if vels == 2:
            return part + lax.ppermute(part, "vel", [(0, 1), (1, 0)])
        return lax.psum(part, "vel")

    x = dist.reshape(own, local)
    up_start = jnp.where(neg == 1, 0, own - 2 * cells)
    down_start = jnp.where(neg == 1, own - cells, 0)
    for turn in range(STEPS):
        both = ("space", "vel")
        upw = lax.ppermute(lax.dynamic_slice_in_dim(x, up_start, 2 * cells, 0), both, upwind)
        dn = lax.ppermute(lax.dynamic_slice_in_dim(x, down_start, cells, 0), both, downwind)
        totals = summed(moments(x, table))
        low = lax.ppermute(totals[:, own - 2 * cells :], "space", rising)
        high = lax.ppermute(totals[:, : 2 * cells], "space", falling)
        low = jnp.where(space > 0, low, totals[:, : 2 * cells])
        high = jnp.where(space < spaces - 1, high, totals[:, own - 2 * cells :])
        extended = jnp.concatenate([low, totals, high], axis=1)
        base, face, part = faces_call(scal, x, upw, dn, extended, mask_slab, table)
        x = renew(scal, boundary, base, face, summed(part), totals, kind_own, mask_own, table)
    return x.reshape(planes, across, height, local)


def solution(mesh):
    spaces, vels = mesh.shape["space"], mesh.shape["vel"]
    return jax.shard_map(
        functools.partial(on_device, spaces=spaces, vels=vels),
        mesh=mesh,
        in_specs=(P("space", None, None, "vel"), P(), P()),
        out_specs=P("space", None, None, "vel"),
        check_vma=False,
    )
```

profile of v0, /device:TPU:23, one launch (start us, length us, event | category | flops | bytes accessed | tf_op | source)
XLA Modules:
  0.0 117.8 jit_solution(10700747931601398377)
XLA Ops:
  0.0 2.1 %constant_dynamic-slice_fusion.3.table_ref = bf16[128,2048]{1,0:T(8,128)(2,1)} fusion(bf16[128,4096]{1,0:T(8,128)(2,1)} %constant.40.clone, s32[]{:T(128)S(6)} %select_n.43), kind=kLoop, calls=%fused_computation.12 | loop fusion | bytes 1048580 | tf_op jit(solution)/shard_map/dynamic_slice | solution.py:398
  2.1 5.8 %moments.2 = f32[16,256]{1,0:T(8,128)} custom-call(f32[256,2048]{1,0:T(8,128)} %bitcast.5, bf16[128,2048]{1,0:T(8,128)(2,1)} %constant_dynamic-slice_fusion.3.table_ref), custom_call_target="tpu_custom_call" | custom-call | tf_op jit(solution)/shard_map/moments/pallas_call | solution.py:494
  7.8 0.2 collective-permute-start.2
  8.1 1.0 constant_dynamic-slice_fusion.5
  9.1 4.0 %collective-permute-start = (f32[128,2048]{1,0:T(8,128)}, f32[128,2048]{1,0:T(8,128)S(1)}, u32[]{:S(2)}, u32[]{:S(2)}) collective-permute-start(f32[128,2048]{1,0:T(8,128)} %constant_dynamic-slice_fusion.5), channel_id=1, source_target_pairs={{2,0},{1,3},{4,2},{3,5},{6,4},{5,7},{8,6},{7,9},{10,8},{9,11},{12,... | collective-permute-start | bytes 3145736 | tf_op jit(solution)/shard_map/ppermute | solution.py:492
  13.1 0.8 constant_dynamic-slice_fusion.4
  14.0 1.9 %collective-permute-start.1 = (f32[64,2048]{1,0:T(8,128)}, f32[64,2048]{1,0:T(8,128)S(1)}, u32[]{:S(2)}, u32[]{:S(2)}) collective-permute-start(f32[64,2048]{1,0:T(8,128)} %constant_dynamic-slice_fusion.4), channel_id=1, source_target_pairs={{0,2},{3,1},{2,4},{5,3},{4,6},{7,5},{6,8},{9,7},{8,10},{11,9},{10,... | collective-permute-start | bytes 1572872 | tf_op jit(solution)/shard_map/ppermute | solution.py:493
  15.9 0.1 fusion
  16.0 0.1 copy.6
  16.1 0.1 convert_element_type.18
  16.2 0.1 constant_dynamic-slice_fusion.2
  16.3 4.5 %collective-permute-start.3 = (f32[16,128]{1,0:T(8,128)S(1)}, f32[16,128]{1,0:T(8,128)S(1)}, u32[]{:S(2)}, u32[]{:S(2)}) collective-permute-start(f32[16,128]{1,0:T(8,128)S(1)} %get-tuple-element.23), channel_id=1, source_target_pairs={{0,2},{2,4},{4,6},{6,8},{8,10},{10,12},{12,14},{14,16},{16,18},{18... | collective-permute-start | bytes 24584 | tf_op jit(solution)/shard_map/ppermute | solution.py:495
  20.8 1.9 %collective-permute-start.4 = (f32[16,128]{1,0:T(8,128)S(1)}, f32[16,128]{1,0:T(8,128)S(1)}, u32[]{:S(2)}, u32[]{:S(2)}) collective-permute-start(f32[16,128]{1,0:T(8,128)S(1)} %get-tuple-element.24), channel_id=1, source_target_pairs={{2,0},{4,2},{6,4},{8,6},{10,8},{12,10},{14,12},{16,14},{18,16},{20... | collective-permute-start | bytes 24584 | tf_op jit(solution)/shard_map/ppermute | solution.py:496
  22.8 0.7 pad_add_fusion.scal_ref
  23.4 1.8 %collective-permute-done.3 = f32[16,128]{1,0:T(8,128)S(1)} collective-permute-done((f32[16,128]{1,0:T(8,128)S(1)}, f32[16,128]{1,0:T(8,128)S(1)}, u32[]{:S(2)}, u32[]{:S(2)}) %collective-permute-start.3) | collective-permute-done | bytes 8224 | tf_op jit(solution)/shard_map/ppermute | solution.py:495
  25.2 1.6 %collective-permute-done.4 = f32[16,128]{1,0:T(8,128)S(1)} collective-permute-done((f32[16,128]{1,0:T(8,128)S(1)}, f32[16,128]{1,0:T(8,128)S(1)}, u32[]{:S(2)}, u32[]{:S(2)}) %collective-permute-start.4) | collective-permute-done | bytes 8224 | tf_op jit(solution)/shard_map/ppermute | solution.py:496
  26.8 0.6 pad_maximum_fusion.tot_ref
  27.4 1.0 broadcast_in_dim.8.mask_ref
  28.4 0.3 copy-done.1
  28.7 13.4 %faces.2 = (f32[256,2048]{1,0:T(8,128)}, f32[688,2048]{1,0:T(8,128)}, f32[16,768]{1,0:T(8,128)}) custom-call(s32[2]{0:T(128)} %pad_add_fusion.scal_ref, f32[256,2048]{1,0:T(8,128)} %bitcast.6, f32[128,2048]{1,0:T(8,128)} %copy-done.1, f32[64,2048]{1,0:T(8,128)} %copy-done.3, f32[16,512]{1,0:T(8,128)} %pad_maximum_fusion.tot_ref, ...), custom_call_target="tpu_custom_call" | custom-call | tf_op jit(solution)/shard_map/faces/pallas_call | solution.py:500
  42.1 1.0 collective-permute-start.5
  43.1 0.1 pad_dynamic-slice_fusion
  43.2 0.1 slice.37
  43.3 0.1 copy.7
  43.4 0.7 reshape.33.kind_ref
  44.1 0.1 copy.8
  44.2 0.1 slice.32
  44.3 1.0 collective-permute-done.5
  45.3 1.4 %add.28.mom_ref = f32[16,768]{1,0:T(8,128)} add(f32[16,768]{1,0:T(8,128)} %get-tuple-element.13, f32[16,768]{1,0:T(8,128)S(1)} %collective-permute-done.5) | non-fusion elementwise | flops 12288 | bytes 147456 | tf_op jit(solution)/shard_map/add | solution.py:484
  46.8 0.7 broadcast_in_dim.9.mask_ref
  47.5 9.1 %renew.2.x_ref = f32[256,2048]{1,0:T(8,128)} custom-call(s32[2]{0:T(128)} %pad_add_fusion.scal_ref, f32[6]{0:T(128)} %bound_ref.3, f32[256,2048]{1,0:T(8,128)} %get-tuple-element.11.base_ref, f32[688,2048]{1,0:T(8,128)} %get-tuple-element.12.face_ref, f32[16,768]{1,0:T(8,128)} %add.28.mom_ref, f32[16,256]{1,0:T(8,128)} %copy-done.5, ...), custom_call_target="tpu_custom_call" | custom-call | tf_op jit(solution)/shard_map/renew/pallas_call | solution.py:501
  56.7 1.3 %constant_dynamic-slice_fusion.1 = f32[128,2048]{1,0:T(8,128)S(1)} fusion(f32[256,2048]{1,0:T(8,128)} %renew.2.x_ref, s32[]{:T(128)S(6)} %select_n.40), kind=kLoop, calls=%fused_computation.10 | loop fusion | bytes 2097156 | tf_op jit(solution)/shard_map/dynamic_slice | solution.py:492
  58.0 4.9 %collective-permute-start.6 = (f32[128,2048]{1,0:T(8,128)S(1)}, f32[128,2048]{1,0:T(8,128)S(1)}, u32[]{:S(2)}, u32[]{:S(2)}) collective-permute-start(f32[128,2048]{1,0:T(8,128)S(1)} %constant_dynamic-slice_fusion.1), channel_id=1, source_target_pairs={{2,0},{1,3},{4,2},{3,5},{6,4},{5,7},{8,6},{7,9},{10,8},{9,11},{12,... | collective-permute-start | bytes 3145736 | tf_op jit(solution)/shard_map/ppermute | solution.py:492
  62.8 5.8 %moments.3 = f32[16,256]{1,0:T(8,128)} custom-call(f32[256,2048]{1,0:T(8,128)} %renew.2.x_ref, bf16[128,2048]{1,0:T(8,128)(2,1)} %constant_dynamic-slice_fusion.3.table_ref), custom_call_target="tpu_custom_call" | custom-call | tf_op jit(solution)/shard_map/moments/pallas_call | solution.py:494
  68.6 5.4 %collective-permute-start.8 = (f32[16,256]{1,0:T(8,128)}, f32[16,256]{1,0:T(8,128)S(1)}, u32[]{:S(2)}, u32[]{:S(2)}) collective-permute-start(f32[16,256]{1,0:T(8,128)} %moments.3), channel_id=1, source_target_pairs={{0,1},{1,0},{2,3},{3,2},{4,5},{5,4},{6,7},{7,6},{8,9},{9,8},{10,11... | collective-permute-start | bytes 49160 | tf_op jit(solution)/shard_map/ppermute | solution.py:484
  74.1 1.1 constant_dynamic-slice_fusion
  75.1 2.2 %collective-permute-start.7 = (f32[64,2048]{1,0:T(8,128)S(1)}, f32[64,2048]{1,0:T(8,128)S(1)}, u32[]{:S(2)}, u32[]{:S(2)}) collective-permute-start(f32[64,2048]{1,0:T(8,128)S(1)} %constant_dynamic-slice_fusion), channel_id=1, source_target_pairs={{0,2},{3,1},{2,4},{5,3},{4,6},{7,5},{6,8},{9,7},{8,10},{11,9},{10,... | collective-permute-start | bytes 1572872 | tf_op jit(solution)/shard_map/ppermute | solution.py:493
  77.4 0.7 add.29.tot_ref
  78.1 4.3 %collective-permute-start.9 = (f32[16,128]{1,0:T(8,128)S(1)}, f32[16,128]{1,0:T(8,128)S(1)}, u32[]{:S(2)}, u32[]{:S(2)}) collective-permute-start(f32[16,128]{1,0:T(8,128)S(1)} %get-tuple-element.19), channel_id=1, source_target_pairs={{0,2},{2,4},{4,6},{6,8},{8,10},{10,12},{12,14},{14,16},{16,18},{18... | collective-permute-start | bytes 24584 | tf_op jit(solution)/shard_map/ppermute | solution.py:495
  82.3 1.9 %collective-permute-start.10 = (f32[16,128]{1,0:T(8,128)S(1)}, f32[16,128]{1,0:T(8,128)S(1)}, u32[]{:S(2)}, u32[]{:S(2)}) collective-permute-start(f32[16,128]{1,0:T(8,128)S(1)} %get-tuple-element.20), channel_id=1, source_target_pairs={{2,0},{4,2},{6,4},{8,6},{10,8},{12,10},{14,12},{16,14},{18,16},{20... | collective-permute-start | bytes 24584 | tf_op jit(solution)/shard_map/ppermute | solution.py:496
  84.3 3.9 %collective-permute-done.10 = f32[16,128]{1,0:T(8,128)S(1)} collective-permute-done((f32[16,128]{1,0:T(8,128)S(1)}, f32[16,128]{1,0:T(8,128)S(1)}, u32[]{:S(2)}, u32[]{:S(2)}) %collective-permute-start.10) | collective-permute-done | bytes 8224 | tf_op jit(solution)/shard_map/ppermute | solution.py:496
  88.2 0.6 pad_maximum_fusion.1.tot_ref
  88.8 0.8 copy-done.4
  89.6 1.0 copy-done.2
  90.6 13.5 %faces.3 = (f32[256,2048]{1,0:T(8,128)}, f32[688,2048]{1,0:T(8,128)}, f32[16,768]{1,0:T(8,128)}) custom-call(s32[2]{0:T(128)} %pad_add_fusion.scal_ref, f32[256,2048]{1,0:T(8,128)} %renew.2.x_ref, f32[128,2048]{1,0:T(8,128)} %copy-done.2, f32[64,2048]{1,0:T(8,128)} %copy-done.4, f32[16,512]{1,0:T(8,128)} %pad_maximum_fusion.1.tot_ref, ...), custom_call_target="tpu_custom_call" | custom-call | tf_op jit(solution)/shard_map/faces/pallas_call | solution.py:500
  104.2 3.1 %collective-permute-done.11 = f32[16,768]{1,0:T(8,128)S(1)} collective-permute-done((f32[16,768]{1,0:T(8,128)}, f32[16,768]{1,0:T(8,128)S(1)}, u32[]{:S(2)}, u32[]{:S(2)}) %collective-permute-start.11) | collective-permute-done | bytes 49184 | tf_op jit(solution)/shard_map/ppermute | solution.py:484
  107.3 1.4 %add.30.mom_ref = f32[16,768]{1,0:T(8,128)} add(f32[16,768]{1,0:T(8,128)} %get-tuple-element.16, f32[16,768]{1,0:T(8,128)S(1)} %collective-permute-done.11) | non-fusion elementwise | flops 12288 | bytes 147456 | tf_op jit(solution)/shard_map/add | solution.py:484
  108.7 9.1 %renew.3 = f32[256,2048]{1,0:T(8,128)} custom-call(s32[2]{0:T(128)} %pad_add_fusion.scal_ref, f32[6]{0:T(128)} %bound_ref.3, f32[256,2048]{1,0:T(8,128)} %get-tuple-element.14.base_ref, f32[688,2048]{1,0:T(8,128)} %get-tuple-element.15.face_ref, f32[16,768]{1,0:T(8,128)} %add.30.mom_ref, f32[16,256]{1,0:T(8,128)} %copy-done.6, s32[1,256]{1,0:T(1,128)} %reshape.33.kind_ref, ...), custom_call_target="tpu_custom_call" | custom-call | tf_op jit(solution)/shard_map/renew/pallas_call | solution.py:501
  (28 shorter events, 0.1 us)
Async XLA Ops:
  0.0 8.1 %copy-start = (f32[4,8,8,2048]{3,2,1,0:T(8,128)S(1)}, f32[4,8,8,2048]{3,2,1,0:T(8,128)}, u32[]{:S(2)}) copy-start(f32[4,8,8,2048]{3,2,1,0:T(8,128)} %param.4) | copy-start | bytes 6291460
  7.8 8.1 %copy-start.7 = (s32[64,8,8]{0,2,1:T(8,128)S(1)}, s32[64,8,8]{0,2,1:T(8,128)}, u32[]{:S(2)}) copy-start(s32[64,8,8]{0,2,1:T(8,128)} %param.5) | copy-start | bytes 49156
  7.8 8.4 %copy-start.8 = (f32[16,256]{1,0:T(8,128)S(1)}, f32[16,256]{1,0:T(8,128)}, u32[]{:S(2)}) copy-start(f32[16,256]{1,0:T(8,128)} %moments.2) | copy-start | bytes 49156
  7.8 8.4 %collective-permute-start.2 = (f32[16,256]{1,0:T(8,128)}, f32[16,256]{1,0:T(8,128)S(1)}, u32[]{:S(2)}, u32[]{:S(2)}) collective-permute-start(f32[16,256]{1,0:T(8,128)} %moments.2), channel_id=1, source_target_pairs={{0,1},{1,0},{2,3},{3,2},{4,5},{5,4},{6,7},{7,6},{8,9},{9,8},{10,11... | collective-permute-start | bytes 49160 | tf_op jit(solution)/shard_map/ppermute | solution.py:484
  9.1 18.3 %collective-permute-start = (f32[128,2048]{1,0:T(8,128)}, f32[128,2048]{1,0:T(8,128)S(1)}, u32[]{:S(2)}, u32[]{:S(2)}) collective-permute-start(f32[128,2048]{1,0:T(8,128)} %constant_dynamic-slice_fusion.5), channel_id=1, source_target_pairs={{2,0},{1,3},{4,2},{3,5},{6,4},{5,7},{8,6},{7,9},{10,8},{9,11},{12,... | collective-permute-start | bytes 3145736 | tf_op jit(solution)/shard_map/ppermute | solution.py:492
  14.0 13.5 %collective-permute-start.1 = (f32[64,2048]{1,0:T(8,128)}, f32[64,2048]{1,0:T(8,128)S(1)}, u32[]{:S(2)}, u32[]{:S(2)}) collective-permute-start(f32[64,2048]{1,0:T(8,128)} %constant_dynamic-slice_fusion.4), channel_id=1, source_target_pairs={{0,2},{3,1},{2,4},{5,3},{4,6},{7,5},{6,8},{9,7},{8,10},{11,9},{10,... | collective-permute-start | bytes 1572872 | tf_op jit(solution)/shard_map/ppermute | solution.py:493
  16.3 25.9 %copy-start.5 = (f32[16,256]{1,0:T(8,128)}, f32[16,256]{1,0:T(8,128)S(1)}, u32[]{:S(2)}) copy-start(f32[16,256]{1,0:T(8,128)S(1)} %add.26.tot_ref) | copy-start | bytes 49156
  16.3 8.9 %collective-permute-start.3 = (f32[16,128]{1,0:T(8,128)S(1)}, f32[16,128]{1,0:T(8,128)S(1)}, u32[]{:S(2)}, u32[]{:S(2)}) collective-permute-start(f32[16,128]{1,0:T(8,128)S(1)} %get-tuple-element.23), channel_id=1, source_target_pairs={{0,2},{2,4},{4,6},{6,8},{8,10},{10,12},{12,14},{14,16},{16,18},{18... | collective-permute-start | bytes 24584 | tf_op jit(solution)/shard_map/ppermute | solution.py:495
  20.8 6.0 %collective-permute-start.4 = (f32[16,128]{1,0:T(8,128)S(1)}, f32[16,128]{1,0:T(8,128)S(1)}, u32[]{:S(2)}, u32[]{:S(2)}) collective-permute-start(f32[16,128]{1,0:T(8,128)S(1)} %get-tuple-element.24), channel_id=1, source_target_pairs={{2,0},{4,2},{6,4},{8,6},{10,8},{12,10},{14,12},{16,14},{18,16},{20... | collective-permute-start | bytes 24584 | tf_op jit(solution)/shard_map/ppermute | solution.py:496
  27.4 1.0 copy-start.3
  27.4 1.3 %copy-start.1 = (f32[128,2048]{1,0:T(8,128)}, f32[128,2048]{1,0:T(8,128)S(1)}, u32[]{:S(2)}) copy-start(f32[128,2048]{1,0:T(8,128)S(1)} %collective-permute-done.upw_ref) | copy-start | bytes 3145732
  42.1 3.2 %collective-permute-start.5 = (f32[16,768]{1,0:T(8,128)}, f32[16,768]{1,0:T(8,128)S(1)}, u32[]{:S(2)}, u32[]{:S(2)}) collective-permute-start(f32[16,768]{1,0:T(8,128)} %get-tuple-element.13), channel_id=1, source_target_pairs={{0,1},{1,0},{2,3},{3,2},{4,5},{5,4},{6,7},{7,6},{8,9},{9,8},{10,11... | collective-permute-start | bytes 147464 | tf_op jit(solution)/shard_map/ppermute | solution.py:484
  58.0 30.9 %collective-permute-start.6 = (f32[128,2048]{1,0:T(8,128)S(1)}, f32[128,2048]{1,0:T(8,128)S(1)}, u32[]{:S(2)}, u32[]{:S(2)}) collective-permute-start(f32[128,2048]{1,0:T(8,128)S(1)} %constant_dynamic-slice_fusion.1), channel_id=1, source_target_pairs={{2,0},{1,3},{4,2},{3,5},{6,4},{5,7},{8,6},{7,9},{10,8},{9,11},{12,... | collective-permute-start | bytes 3145736 | tf_op jit(solution)/shard_map/ppermute | solution.py:492
  68.6 8.7 %collective-permute-start.8 = (f32[16,256]{1,0:T(8,128)}, f32[16,256]{1,0:T(8,128)S(1)}, u32[]{:S(2)}, u32[]{:S(2)}) collective-permute-start(f32[16,256]{1,0:T(8,128)} %moments.3), channel_id=1, source_target_pairs={{0,1},{1,0},{2,3},{3,2},{4,5},{5,4},{6,7},{7,6},{8,9},{9,8},{10,11... | collective-permute-start | bytes 49160 | tf_op jit(solution)/shard_map/ppermute | solution.py:484
  75.1 13.7 %collective-permute-start.7 = (f32[64,2048]{1,0:T(8,128)S(1)}, f32[64,2048]{1,0:T(8,128)S(1)}, u32[]{:S(2)}, u32[]{:S(2)}) collective-permute-start(f32[64,2048]{1,0:T(8,128)S(1)} %constant_dynamic-slice_fusion), channel_id=1, source_target_pairs={{0,2},{3,1},{2,4},{5,3},{4,6},{7,5},{6,8},{9,7},{8,10},{11,9},{10,... | collective-permute-start | bytes 1572872 | tf_op jit(solution)/shard_map/ppermute | solution.py:493
  78.1 26.0 %copy-start.6 = (f32[16,256]{1,0:T(8,128)}, f32[16,256]{1,0:T(8,128)S(1)}, u32[]{:S(2)}) copy-start(f32[16,256]{1,0:T(8,128)S(1)} %add.29.tot_ref) | copy-start | bytes 49156
  78.1 6.2 %collective-permute-start.9 = (f32[16,128]{1,0:T(8,128)S(1)}, f32[16,128]{1,0:T(8,128)S(1)}, u32[]{:S(2)}, u32[]{:S(2)}) collective-permute-start(f32[16,128]{1,0:T(8,128)S(1)} %get-tuple-element.19), channel_id=1, source_target_pairs={{0,2},{2,4},{4,6},{6,8},{8,10},{10,12},{12,14},{14,16},{16,18},{18... | collective-permute-start | bytes 24584 | tf_op jit(solution)/shard_map/ppermute | solution.py:495
  82.3 5.9 %collective-permute-start.10 = (f32[16,128]{1,0:T(8,128)S(1)}, f32[16,128]{1,0:T(8,128)S(1)}, u32[]{:S(2)}, u32[]{:S(2)}) collective-permute-start(f32[16,128]{1,0:T(8,128)S(1)} %get-tuple-element.20), channel_id=1, source_target_pairs={{2,0},{4,2},{6,4},{8,6},{10,8},{12,10},{14,12},{16,14},{18,16},{20... | collective-permute-start | bytes 24584 | tf_op jit(solution)/shard_map/ppermute | solution.py:496
  88.8 0.8 copy-start.4
  89.6 1.0 copy-start.2
  104.1 3.2 %collective-permute-start.11 = (f32[16,768]{1,0:T(8,128)}, f32[16,768]{1,0:T(8,128)S(1)}, u32[]{:S(2)}, u32[]{:S(2)}) collective-permute-start(f32[16,768]{1,0:T(8,128)} %get-tuple-element.16), channel_id=1, source_target_pairs={{0,1},{1,0},{2,3},{3,2},{4,5},{5,4},{6,7},{7,6},{8,9},{9,8},{10,11... | collective-permute-start | bytes 147464 | tf_op jit(solution)/shard_map/ppermute | solution.py:484
where the time goes:
time: 119 us; the launch traced here: 118 us
  Pallas kernels  56.7 us (48%)
  starting transfers between devices  32.4 us (27%)
  local copies, waits for them, and re-layouts  11.5 us (10%)
  waiting for transfers between devices  11.5 us (10%)
  other arithmetic  5.53 us (5%)
    pallas_call x2, Pallas kernels, on_device(): base, face, part = faces_call(scal, x, upw, dn, extended, mask_slab, table)  26.9 us
    pallas_call x2, Pallas kernels, on_device(): renew(scal, boundary, base, face, summed(part), totals, kind_own, mask_ow...  18.2 us
    pallas_call x2, Pallas kernels, on_device(): totals = summed(moments(x, table))  11.5 us
    ppermute x2, starting transfers between devices, on_device(): lax.ppermute(lax.dynamic_slice_in_dim(x, up_start, 2 * cells, 0), both, u...  8.87 us
    ppermute x2, starting transfers between devices, on_device(): low = lax.ppermute(totals[:, own - 2 * cells:], 'space', rising)  8.8 us
    ppermute x4, starting transfers between devices, summed(): return part + lax.ppermute(part, 'vel', [(0, 1), (1, 0)])  6.74 us
    ppermute x2, waiting for transfers between devices, on_device(): high = lax.ppermute(totals[:, :2 * cells], 'space', falling)  5.54 us
    ppermute x4, waiting for transfers between devices, summed(): return part + lax.ppermute(part, 'vel', [(0, 1), (1, 0)])  4.17 us
  transfers between devices with their start and end apart: 12, of which 5 were waited for; matrix products, arithmetic and copies ran while one was open for 6% of the time, Pallas kernels for 5%

commit v1 on v0

v1 whole, which is shorter than its diff:
```python
import functools
import math

import jax
import jax.numpy as jnp
import numpy as np
from jax import lax
from jax.experimental import pallas as pl
from jax.experimental.pallas import tpu as pltpu
from jax.sharding import PartitionSpec as P

NODES = 16
STEPS = 2
PRANDTL = 2.0 / 3.0
OMEGA = 0.81
MU_REF = 0.1
DT = 0.1
HALF = 0.05
VMAX = 5.0
SPACING = 2.0 * VMAX / NODES
UNIT = 0.5 * SPACING
WEIGHT = SPACING**3 / (2.0 * math.pi) ** 1.5
LOG2E = 1.4426950408889634
COLS = 16
TILE = NODES * NODES
ROWS = 8
HALFTILE = 128
VMEM_LIMIT = 24 * 2**20


def node_table():
    number = np.arange(NODES**3)
    digits = (number // (NODES * NODES), number // NODES % NODES, number % NODES)
    m = [2 * d + 1 - NODES for d in digits]
    n = m[0] * m[0] + m[1] * m[1] + m[2] * m[2]
    third = [c * n for c in m]
    high = [((v + 32) // 64) * 64 for v in third]
    low = [v - h for v, h in zip(third, high)]
    base = [np.ones_like(n), *m, m[0] * m[0], m[1] * m[1], m[2] * m[2]]
    base += [m[0] * m[1], m[0] * m[2], m[1] * m[2], *high, *low]
    table = np.zeros((HALFTILE, NODES**3), np.float32)
    for part in range(3):
        table[part * COLS : (part + 1) * COLS] = np.stack(base)
    return jnp.asarray(table, jnp.bfloat16)


def dot_nt(a, b):
    return lax.dot_general(a, b, (((1,), (1,)), ((), ())), preferred_element_type=jnp.float32)


def dot_nn(a, b):
    return lax.dot_general(a, b, (((1,), (0,)), ((), ())), preferred_element_type=jnp.float32)


def split(value):
    high = value.astype(jnp.bfloat16)
    low = (value - high.astype(jnp.float32)).astype(jnp.bfloat16)
    return high, low


def state_of(t):
    density = t[0]
    second_unit = UNIT * UNIT
    velocity = [UNIT * t[1 + e] / density for e in range(3)]
    second = (
        (second_unit * t[4], second_unit * t[7], second_unit * t[8]),
        (second_unit * t[7], second_unit * t[5], second_unit * t[9]),
        (second_unit * t[8], second_unit * t[9], second_unit * t[6]),
    )
    trace = second[0][0] + second[1][1] + second[2][2]
    speed_sq = velocity[0] * velocity[0] + velocity[1] * velocity[1] + velocity[2] * velocity[2]
    temper = (trace / density - speed_sq) / 3.0
    heat = [
        0.5
        * (
            (UNIT**3) * (t[10 + e] + t[13 + e])
            - 2.0
            * (
                second[e][0] * velocity[0]
                + second[e][1] * velocity[1]
                + second[e][2] * velocity[2]
            )
            - velocity[e] * trace
            + 2.0 * density * velocity[e] * speed_sq
        )
        for e in range(3)
    ]
    return density, velocity, temper, heat


def relaxation(density, temper):
    return MU_REF * jnp.exp(OMEGA * jnp.log(temper)) / (density * temper)


def exponent_coefs(velocity, temper):
    g = -0.5 * LOG2E / temper
    speed_sq = velocity[0] * velocity[0] + velocity[1] * velocity[1] + velocity[2] * velocity[2]
    square = g * (UNIT * UNIT)
    zero = jnp.zeros_like(g)
    linear = [(-2.0 * UNIT) * g * velocity[e] for e in range(3)]
    return [g * speed_sq, *linear, square, square, square] + [zero] * 9


def shakhov_coefs(amplitude, density, velocity, temper, heat):
    factor = (1.0 - PRANDTL) / (5.0 * density * temper * temper)
    af = amplitude * factor
    inverse = 1.0 / temper
    along = velocity[0] * heat[0] + velocity[1] * heat[1] + velocity[2] * heat[2]
    speed_sq = velocity[0] * velocity[0] + velocity[1] * velocity[1] + velocity[2] * velocity[2]
    a2 = (UNIT * UNIT) * inverse
    b = [(-2.0 * UNIT) * velocity[e] * inverse for e in range(3)]
    c = speed_sq * inverse - 5.0
    kq = [UNIT * heat[e] for e in range(3)]
    cubic = [af * (kq[e] * a2) for e in range(3)]
    return [
        amplitude - af * (along * c),
        *[af * (kq[e] * c - along * b[e]) for e in range(3)],
        *[af * (kq[e] * b[e] - along * a2) for e in range(3)],
        af * (kq[0] * b[1] + kq[1] * b[0]),
        af * (kq[0] * b[2] + kq[2] * b[0]),
        af * (kq[1] * b[2] + kq[2] * b[1]),
        *cubic,
        *cubic,
    ]


def transposed_parts(coefs, extras, work):
    work[...] = jnp.zeros(work.shape, jnp.float32)
    for row, value in enumerate(coefs):
        high = value.astype(jnp.bfloat16).astype(jnp.float32)
        rest = value - high
        middle = rest.astype(jnp.bfloat16).astype(jnp.float32)
        work[row : row + 1, :] = high
        work[COLS + row : COLS + row + 1, :] = middle
        work[2 * COLS + row : 2 * COLS + row + 1, :] = rest - middle
    for row, value in enumerate(extras):
        work[3 * COLS + row : 3 * COLS + row + 1, :] = value
    return jnp.transpose(work[...], (1, 0))


def spread_column(matrix, extra=0):
    at = 3 * COLS + extra
    return jnp.broadcast_to(matrix[:, at : at + 1], (matrix.shape[0], HALFTILE))


def tile_lanes(n):
    return pl.ds(pl.multiple_of(n * TILE, TILE), TILE)


def twice(value):
    return jnp.concatenate([value, value], axis=1)


def lane_speeds(shape):
    lane = lax.broadcasted_iota(jnp.int32, shape, 1)
    along_y = (2 * (lane // NODES) + 1 - NODES).astype(jnp.float32) * UNIT
    along_z = (2 * (lane % NODES) + 1 - NODES).astype(jnp.float32) * UNIT
    return along_y, along_z


def add_sends(scal_ref, x_ref, up_ref, down_ref, lanes):
    inner = down_ref.shape[0]
    far = pl.multiple_of(scal_ref[2], ROWS)
    near = pl.multiple_of(scal_ref[3], ROWS)
    down = pl.multiple_of(scal_ref[6], ROWS)
    up_ref[:inner, lanes] = x_ref[pl.ds(far, inner), lanes]
    up_ref[inner:, lanes] = x_ref[pl.ds(near, up_ref.shape[0] - inner), lanes]
    down_ref[:, lanes] = x_ref[pl.ds(down, inner), lanes]


def unroll_of(tiles):
    return 2 if tiles % 2 == 0 else 1


def moments_kernel(
    scal_ref, x_ref, kind_ref, table_ref, out_ref, up_ref, down_ref, mask_ref, acc_ref, work_ref
):
    acc_ref[...] = jnp.zeros_like(acc_ref)

    @pl.loop(0, x_ref.shape[1] // TILE)
    def _(n):
        lanes = tile_lanes(n)
        high, low = split(x_ref[:, lanes])
        table = table_ref[:, tile_lanes(scal_ref[1] + n)]
        acc_ref[...] += dot_nt(high, table) + dot_nt(low, table)
        add_sends(scal_ref, x_ref, up_ref, down_ref, lanes)

    out_ref[...] = WEIGHT * jnp.transpose(acc_ref[...], (1, 0))[:COLS]
    fluid = (kind_ref[...] == 1).astype(jnp.float32)
    mask_ref[...] = spread_column(transposed_parts([], [fluid], work_ref))


def cell_coefs(t):
    density, velocity, temper, heat = state_of(t)
    tau = relaxation(density, temper)
    heat = [q / (1.0 + DT * PRANDTL / (2.0 * tau)) for q in heat]
    divide = 1.0 / (2.0 * tau + DT)
    alpha = (2.0 * tau - HALF) * divide
    beta = (3.0 * HALF) * divide
    amplitude = beta * (density / (temper * jnp.sqrt(temper)))
    poly = shakhov_coefs(amplitude, density, velocity, temper, heat)
    return exponent_coefs(velocity, temper), poly, alpha


def middle(a, b):
    return jnp.maximum(jnp.minimum(a, b), jnp.minimum(jnp.maximum(a, b), 0.0))


class Lanes:
    def __init__(self):
        along_y, along_z = lane_speeds((ROWS, TILE))
        lane = lax.broadcasted_iota(jnp.int32, (ROWS, TILE), 1)
        self.z_minus = (lane % NODES) < NODES // 2
        self.ky = HALF * along_y
        self.kz = HALF * along_z
        self.hy = jnp.where(lane < HALFTILE, -0.5, 0.5)
        self.hz = jnp.where(self.z_minus, -0.5, 0.5)


def put_faces(face_ref, part_ref, lanes, first, row, pair):
    both = jnp.concatenate(pair, axis=0)
    high, low = split(both)
    rows = slice(row, row + 2 * ROWS)
    face_ref[rows, lanes] = both
    part_ref[rows, first : first + TILE] = high
    part_ref[rows, first + TILE : first + 2 * TILE] = low


def plane_faces(col, ahead, behind, mask_of, kx, hx, node, put, rows_x, rows_y, rows_z):
    values = {0: col(0), 1: col(1)}
    diff = values[1] - values[0]
    own = rows_y is not None
    fx, fy, fz = {}, {0: values[0]}, {}
    for y in range(1, ROWS - 1):
        here = values[y]
        values[y + 1] = col(y + 1)
        back, diff = diff, values[y + 1] - here
        mask = mask_of(y)
        slope_y = middle(diff, back) * mask
        slope_x = mask * middle(ahead(y) - here, here - behind(y))
        step = here - pltpu.roll(here, 1, 0)
        slope_z = middle(pltpu.roll(step, ROWS - 1, 0), step) * mask
        centre = here - (kx * slope_x + node.ky * slope_y + node.kz * slope_z)
        fx[y] = centre + hx * slope_x
        if own:
            fy[y] = centre + node.hy * slope_y
            side = centre + node.hz * slope_z
            fz[y] = jnp.where(node.z_minus, side, pltpu.roll(side, 1, 0))
    for i in range((ROWS - 2) // 2):
        put(rows_x + 16 * i, [fx[1 + 2 * i], fx[2 + 2 * i]])
    if own:
        fy[ROWS - 1] = values[ROWS - 1]
        gy = [fy[0]]
        for j in range(1, ROWS):
            gy.append(jnp.concatenate([fy[j][:, :HALFTILE], fy[j - 1][:, HALFTILE:]], axis=1))
        for i in range(ROWS // 2):
            put(rows_y + 16 * i, [gy[2 * i], gy[2 * i + 1]])
        for i in range((ROWS - 2) // 2):
            put(rows_z + 16 * i, [fz[1 + 2 * i], fz[2 + 2 * i]])


def x_factors(scal_ref, n):
    along_x = (2 * (scal_ref[1] + n) + 1 - NODES).astype(jnp.float32) * UNIT
    return HALF * along_x, jnp.where(along_x > 0, 0.5, -0.5)


def stacked_tables(tables):
    return jnp.concatenate([t for t in tables for _ in range(2)], axis=1)


def inner_kernel(
    scal_ref, x_ref, tot_ref, mask_ref, table_ref,
    cell_ref, face_ref, acc_ref,
    work_ref, lhs_ref, alpha_ref, part_ref, *res_refs,
    planes,
):
    cells = ROWS * ROWS
    inner = (ROWS - 2) * ROWS
    own = planes * cells
    count = planes - 2
    unroll = len(res_refs)
    exponent, poly, alpha = cell_coefs([tot_ref[i : i + 1, :] for i in range(COLS)])
    turned = transposed_parts(exponent, [alpha], work_ref)
    lhs_ref[0:own, :] = turned.astype(jnp.bfloat16)
    alpha_ref[...] = spread_column(turned)
    lhs_ref[own : 2 * own, :] = transposed_parts(poly, [], work_ref).astype(jnp.bfloat16)
    acc_ref[...] = jnp.zeros_like(acc_ref)
    node = Lanes()

    @pl.loop(0, x_ref.shape[1] // (TILE * unroll))
    def _(m):
        tables = []
        for k, res_ref in enumerate(res_refs):
            n = m * unroll + k
            lanes = tile_lanes(n)
            table = table_ref[:, tile_lanes(scal_ref[1] + n)]
            tables.append(table)
            res_ref[...] = dot_nn(lhs_ref[...], table)
        for k, res_ref in enumerate(res_refs):
            n = m * unroll + k
            lanes = tile_lanes(n)
            kx, hx = x_factors(scal_ref, n)
            for r in range(0, own, 16):
                rows = slice(r, r + 16)
                cell_ref[rows, lanes] = twice(alpha_ref[rows, :]) * x_ref[rows, lanes] + jnp.exp2(
                    res_ref[rows, :]
                ) * res_ref[own + r : own + r + 16, :]
            put = functools.partial(put_faces, face_ref, part_ref, lanes, 2 * TILE * k)
            for i in range(count):
                base = (i + 1) * cells

                def col(y, base=base):
                    return cell_ref[base + y * ROWS : base + (y + 1) * ROWS, lanes]

                def mask_of(y, base=base):
                    at = 2 * cells + base + y * ROWS
                    return twice(mask_ref[at : at + ROWS, :])

                plane_faces(
                    col,
                    lambda y, base=base: col(y, base + cells),
                    lambda y, base=base: col(y, base - cells),
                    mask_of, kx, hx, node, put,
                    i * inner, count * inner + i * cells, count * (inner + cells) + i * inner,
                )
        acc_ref[...] += dot_nt(part_ref[...], stacked_tables(tables))


def outer_kernel(
    scal_ref, cell_ref, upw_ref, dn_ref, below_ref, above_ref, tot_ref, mask_ref, table_ref,
    inacc_ref,
    face_ref, mom_ref,
    ext_ref, work_ref, full_ref, lhs_ref, alpha_ref, slab_ref, part_ref, acc_ref, sum_ref,
    *res_refs, planes,
):
    neg = scal_ref[0]
    cells = ROWS * ROWS
    inner = (ROWS - 2) * ROWS
    own = planes * cells
    count = planes - 2
    ghosts = cells + 2 * inner
    unroll = len(res_refs)

    ext_ref[:, : 2 * cells] = jnp.where(scal_ref[4] > 0, below_ref[...], tot_ref[:, : 2 * cells])
    ext_ref[:, 2 * cells :] = jnp.where(
        scal_ref[5] > 0, above_ref[...], tot_ref[:, own - 2 * cells :]
    )
    exponent, poly, alpha = cell_coefs([ext_ref[i : i + 1, :] for i in range(COLS)])
    near = pl.ds(pl.multiple_of((1 + neg) * cells, ROWS), cells)
    far = pl.ds(pl.multiple_of(3 * neg * cells + ROWS, ROWS), inner)
    down = pl.ds(pl.multiple_of((2 - neg) * cells + ROWS, ROWS), inner)

    def gather():
        return jnp.concatenate([full_ref[far, :], full_ref[near, :], full_ref[down, :]], axis=0)

    full_ref[...] = transposed_parts(exponent, [alpha], work_ref)
    turned = gather()
    lhs_ref[0:ghosts, :] = turned.astype(jnp.bfloat16)
    alpha_ref[...] = spread_column(turned)
    full_ref[...] = transposed_parts(poly, [], work_ref)
    lhs_ref[ghosts : 2 * ghosts, :] = gather().astype(jnp.bfloat16)
    acc_ref[...] = jnp.zeros_like(acc_ref)
    node = Lanes()
    minus = neg > 0
    near_mask = pl.multiple_of((1 + (planes + 1) * neg) * cells, ROWS)

    @pl.loop(0, cell_ref.shape[1] // (TILE * unroll))
    def _(m):
        tables = []
        for k, res_ref in enumerate(res_refs):
            n = m * unroll + k
            table = table_ref[:, tile_lanes(scal_ref[1] + n)]
            tables.append(table)
            res_ref[...] = dot_nn(lhs_ref[...], table)
        for k, res_ref in enumerate(res_refs):
            n = m * unroll + k
            lanes = tile_lanes(n)
            kx, hx = x_factors(scal_ref, n)
            for r in range(0, ghosts, 16):
                rows = slice(r, r + 16)
                if r < inner + cells:
                    f = upw_ref[rows, lanes]
                else:
                    f = dn_ref[r - inner - cells : r - inner - cells + 16, lanes]
                slab_ref[rows, k * TILE : (k + 1) * TILE] = twice(alpha_ref[rows, :]) * f + jnp.exp2(
                    res_ref[rows, :]
                ) * res_ref[ghosts + r : ghosts + r + 16, :]
            put = functools.partial(put_faces, face_ref, part_ref, lanes, 2 * TILE * k)

            def ghost(first, y):
                at = first + y * ROWS
                return slab_ref[at : at + ROWS, k * TILE : (k + 1) * TILE]

            far_at = functools.partial(ghost, -ROWS)
            near_at = functools.partial(ghost, inner)
            down_at = functools.partial(ghost, inner + cells - ROWS)

            def cell(plane, y):
                at = plane * cells + y * ROWS
                return cell_ref[at : at + ROWS, lanes]

            def cell_mask(plane, y):
                at = (2 + plane) * cells + y * ROWS
                return twice(mask_ref[at : at + ROWS, :])

            def ghost_mask(y):
                at = pl.multiple_of(near_mask + y * ROWS, ROWS)
                return twice(mask_ref[pl.ds(at, ROWS), :])

            end = planes - 1
            plane_faces(
                near_at,
                lambda y: jnp.where(minus, cell(end, y), cell(0, y)),
                far_at,
                ghost_mask, jnp.abs(kx), 0.5, node, put, 0, None, None,
            )
            plane_faces(
                functools.partial(cell, 0),
                functools.partial(cell, 1),
                lambda y: jnp.where(minus, down_at(y), near_at(y)),
                functools.partial(cell_mask, 0), kx, hx, node, put,
                inner, 3 * inner, 3 * inner + 2 * cells,
            )
            plane_faces(
                functools.partial(cell, end),
                lambda y: jnp.where(minus, near_at(y), down_at(y)),
                functools.partial(cell, end - 1),
                functools.partial(cell_mask, end), kx, hx, node, put,
                2 * inner, 3 * inner + cells, 4 * inner + 2 * cells,
            )
        acc_ref[...] += dot_nt(part_ref[...], stacked_tables(tables))

    face_y = (planes + 1) * inner
    face_z = face_y + planes * cells
    used = face_z + planes * inner
    if sum_ref.shape[0] > used:
        sum_ref[used:, :] = jnp.zeros((sum_ref.shape[0] - used, HALFTILE), jnp.float32)

    def place(row, size, source, at):
        sum_ref[pl.ds(pl.multiple_of(row, ROWS), size), :] = source[at : at + size, :]

    place(planes * neg * inner, inner, acc_ref, 0)
    for p in range(planes):
        outer = p in (0, planes - 1)
        source = acc_ref if outer else inacc_ref
        i = (0 if p == 0 else 1) if outer else p - 1
        size = 2 if outer else count
        skip = inner if outer else 0
        place((p + 1 - neg) * inner, inner, source, skip + i * inner)
        place(face_y + p * cells, cells, source, skip + size * inner + i * cells)
        place(face_z + p * inner, inner, source, skip + size * (inner + cells) + i * inner)
    mom_ref[...] = WEIGHT * jnp.transpose(sum_ref[...], (1, 0))[:COLS]


def renew_kernel(
    scal_ref, bound_ref, x_ref, cell_ref, in_ref, edge_ref, mom_ref, peer_ref, tot_ref, kind_ref,
    mask_ref, table_ref,
    *refs, planes, last, unroll,
):
    if last:
        out_ref, *refs = refs
    else:
        out_ref, next_ref, up_ref, down_ref, *refs = refs
    work_ref, wide_ref, lhs_ref, keep_ref, amp_ref, acc_ref, part_ref, *refs = refs
    res_refs, flux_refs = refs[:unroll], refs[unroll:]
    minus = scal_ref[0] > 0
    cells = ROWS * ROWS
    inner = (ROWS - 2) * ROWS
    count = planes - 2
    face_y = (planes + 1) * inner
    face_z = face_y + planes * cells
    faces = face_z + planes * inner
    own = planes * cells

    t = [mom_ref[i : i + 1, :] + peer_ref[i : i + 1, :] for i in range(COLS)]
    density, velocity, temper, heat = state_of(t)
    tau = relaxation(density, temper)
    heat = [2.0 * tau * q / (2.0 * tau + HALF * PRANDTL) for q in heat]
    divide = 1.0 / (2.0 * tau + HALF)
    keep = 2.0 * tau * divide
    amplitude = (HALF * divide) * (density / (temper * jnp.sqrt(temper)))
    turned = transposed_parts(exponent_coefs(velocity, temper), [keep], wide_ref)[:faces]
    lhs_ref[0:faces, :] = turned.astype(jnp.bfloat16)
    keep_ref[...] = spread_column(turned)
    turned = transposed_parts(
        shakhov_coefs(amplitude, density, velocity, temper, heat), [], wide_ref
    )[:faces]
    lhs_ref[faces : 2 * faces, :] = turned.astype(jnp.bfloat16)

    density = tot_ref[0:1, :]
    kind = kind_ref[:, 2 * cells : 2 * cells + own]
    inlet, outlet = kind == 2, kind == 3
    moving = [
        jnp.where(outlet, UNIT * tot_ref[1 + e : 2 + e, :] / density, 0.0) for e in range(3)
    ]
    moving[0] = jnp.where(inlet, bound_ref[1], moving[0])
    dense = jnp.where(inlet, bound_ref[0], jnp.where(outlet, bound_ref[3], density))
    warm = jnp.where(inlet, bound_ref[2], jnp.where(outlet, bound_ref[4], bound_ref[5]))
    amplitude = dense / (warm * jnp.sqrt(warm))
    turned = transposed_parts(exponent_coefs(moving, warm), [amplitude], work_ref)
    lhs_ref[2 * faces : 2 * faces + own, :] = turned.astype(jnp.bfloat16)
    amp_ref[...] = spread_column(turned)
    acc_ref[...] = jnp.zeros_like(acc_ref)

    along_y, along_z = lane_speeds((ROWS, TILE))
    hy = DT * along_y
    hz = DT * along_z

    def along_x_source(plane):
        if plane in (-1, planes):
            return edge_ref, 0
        if plane in (0, planes - 1):
            return edge_ref, inner if plane == 0 else 2 * inner
        return in_ref, (plane - 1) * inner

    def face_rows(r, lanes):
        rows = 2 * ROWS

        def load(ref, at):
            return ref[at : at + rows, lanes]

        if r < face_y:
            w, rest = divmod(r, inner)
            ref, at = along_x_source(w)
            other, there = along_x_source(w - 1)
            return jnp.where(minus, load(ref, at + rest), load(other, there + rest))
        size, start = (cells, face_y) if r < face_z else (inner, face_z)
        p, rest = divmod(r - start, size)
        outer = p in (0, planes - 1)
        i = (0 if p == 0 else 1) if outer else p - 1
        many, skip = (2, inner) if outer else (count, 0)
        before = skip + many * (inner if r < face_z else inner + cells)
        return load(edge_ref if outer else in_ref, before + i * size + rest)

    @pl.loop(0, x_ref.shape[1] // (TILE * unroll))
    def _(m):
        tables = []
        for k, res_ref in enumerate(res_refs):
            n = m * unroll + k
            table = table_ref[:, tile_lanes(scal_ref[1] + n)]
            tables.append(table)
            res_ref[...] = dot_nn(lhs_ref[...], table)
        for k, (res_ref, flux_ref) in enumerate(zip(res_refs, flux_refs)):
            n = m * unroll + k
            lanes = tile_lanes(n)
            digit = scal_ref[1] + n
            hx = (2 * digit + 1 - NODES).astype(jnp.float32) * (UNIT * DT)
            for r in range(0, faces, 16):
                rows = slice(r, r + 16)
                poly = res_ref[faces + r : faces + r + 16, :]
                flux_ref[rows, :] = (
                    twice(keep_ref[rows, :]) * face_rows(r, lanes) + jnp.exp2(res_ref[rows, :]) * poly
                )
            for p in range(planes):
                done = []
                for y in range(ROWS):
                    at = p * cells + y * ROWS
                    rows = slice(at, at + ROWS)
                    value = twice(amp_ref[rows, :]) * jnp.exp2(
                        res_ref[2 * faces + at : 2 * faces + at + ROWS, :]
                    )
                    if 0 < y < ROWS - 1:
                        ax = p * inner + (y - 1) * ROWS
                        ay = face_y + at
                        az = face_z + ax
                        along = (
                            flux_ref[ax + inner : ax + inner + ROWS, :]
                            - flux_ref[ax : ax + ROWS, :]
                        )
                        across = (
                            flux_ref[ay + ROWS : ay + 2 * ROWS, :] - flux_ref[ay : ay + ROWS, :]
                        )
                        low = flux_ref[az : az + ROWS, :]
                        rise = pltpu.roll(low, ROWS - 1, 0) - low
                        plus = (4.0 / 3.0) * cell_ref[rows, lanes] - (1.0 / 3.0) * x_ref[rows, lanes]
                        fresh = plus - (hx * along + hy * across + hz * rise)
                        at += 2 * cells
                        mask = twice(mask_ref[at : at + ROWS, :]) > 0.0
                        value = jnp.where(mask, fresh, value)
                    done.append(value)
                    if y % 2:
                        both = jnp.concatenate(done, axis=0)
                        rows = slice(p * cells + (y - 1) * ROWS, p * cells + (y + 1) * ROWS)
                        out_ref[rows, lanes] = both
                        if not last:
                            high, low = split(both)
                            first = 2 * TILE * k
                            part_ref[rows, first : first + TILE] = high
                            part_ref[rows, first + TILE : first + 2 * TILE] = low
                        done = []
        if not last:
            acc_ref[...] += dot_nt(part_ref[...], stacked_tables(tables))
            for k in range(unroll):
                add_sends(scal_ref, out_ref, up_ref, down_ref, tile_lanes(m * unroll + k))

    if not last:
        next_ref[...] = WEIGHT * jnp.transpose(acc_ref[...], (1, 0))[:COLS]


def on_device(dist, cell_type, boundary, *, spaces, vels):
    planes, across, height, local = dist.shape
    cells = across * height
    own = planes * cells
    inner = cells - 2 * height
    faces = (planes + 1) * inner + planes * cells + planes * inner
    padded = -(-faces // 128) * 128
    extended = own + 4 * cells
    ghosts = cells + 2 * inner
    faces_in = (planes - 2) * (2 * inner + cells)
    faces_edge = inner + 2 * (2 * inner + cells)
    tiles = local // TILE
    unroll = unroll_of(tiles)
    space, vel = lax.axis_index("space"), lax.axis_index("vel")
    neg = (vel < vels // 2).astype(jnp.int32)
    scal = jnp.stack(
        [
            neg,
            vel * tiles,
            height + jnp.where(neg == 1, cells, own - 2 * cells),
            jnp.where(neg == 1, 0, own - cells),
            (space > 0).astype(jnp.int32),
            (space < spaces - 1).astype(jnp.int32),
            height + jnp.where(neg == 1, own - cells, 0),
        ]
    ).astype(jnp.int32)
    table = node_table()
    kinds = jnp.pad(cell_type, ((2, 2), (0, 0), (0, 0)))
    kinds = lax.dynamic_slice_in_dim(kinds, space * planes, planes + 4, 0).reshape(1, extended)

    smem = pl.BlockSpec(memory_space=pltpu.SMEM)
    vmem = pl.BlockSpec(memory_space=pltpu.VMEM)
    f32, bf16 = jnp.float32, jnp.bfloat16
    shape = lambda *dims: jax.ShapeDtypeStruct(dims, f32)
    scratch = lambda *dims: pltpu.VMEM(dims, f32)
    packed = lambda *dims: pltpu.VMEM(dims, bf16)
    params = pltpu.CompilerParams(vmem_limit_bytes=VMEM_LIMIT)
    cost = lambda us: pl.CostEstimate(
        flops=int(us * 1e9), bytes_accessed=1 << 20, transcendentals=0
    )
    sends = [shape(COLS, own), shape(inner + cells, local), shape(inner, local)]

    moments = pl.pallas_call(
        moments_kernel,
        in_specs=[smem] + [vmem] * 3,
        out_specs=[vmem] * 4,
        out_shape=sends + [shape(extended, HALFTILE)],
        scratch_shapes=[scratch(own, HALFTILE), scratch(HALFTILE, extended)],
        compiler_params=params,
        cost_estimate=cost(2),
        name="moments",
    )
    inside = pl.pallas_call(
        functools.partial(inner_kernel, planes=planes),
        in_specs=[smem] + [vmem] * 4,
        out_specs=[vmem] * 3,
        out_shape=[shape(own, local), shape(faces_in, local), shape(faces_in, HALFTILE)],
        scratch_shapes=[
            scratch(HALFTILE, own),
            packed(2 * own, HALFTILE),
            scratch(own, HALFTILE),
            packed(faces_in, 2 * TILE * unroll),
        ]
        + [scratch(2 * own, TILE)] * unroll,
        compiler_params=params,
        cost_estimate=cost(6),
        name="facesin",
    )
    outside = pl.pallas_call(
        functools.partial(outer_kernel, planes=planes),
        in_specs=[smem] + [vmem] * 9,
        out_specs=[vmem] * 2,
        out_shape=[shape(faces_edge, local), shape(COLS, padded)],
        scratch_shapes=[
            scratch(COLS, 4 * cells),
            scratch(HALFTILE, 4 * cells),
            scratch(4 * cells, HALFTILE),
            packed(2 * ghosts, HALFTILE),
            scratch(ghosts, HALFTILE),
            scratch(ghosts, TILE * unroll),
            packed(faces_edge, 2 * TILE * unroll),
            scratch(faces_edge, HALFTILE),
            scratch(padded, HALFTILE),
        ]
        + [scratch(2 * ghosts, TILE)] * unroll,
        compiler_params=params,
        cost_estimate=cost(6),
        name="faceb",
    )

    def renew(last):
        return pl.pallas_call(
            functools.partial(renew_kernel, planes=planes, last=last, unroll=unroll),
            in_specs=[smem, smem] + [vmem] * 10,
            out_specs=[vmem] * (1 if last else 4),
            out_shape=[shape(own, local)] + ([] if last else sends),
            scratch_shapes=[
                scratch(HALFTILE, own),
                scratch(HALFTILE, padded),
                packed(2 * faces + own, HALFTILE),
                scratch(faces, HALFTILE),
                scratch(own, HALFTILE),
                scratch(own, HALFTILE),
                packed(own, 2 * TILE * unroll),
            ]
            + [scratch(2 * faces + own, TILE)] * unroll
            + [scratch(faces, TILE)] * unroll,
            compiler_params=params,
            cost_estimate=cost(6),
            name="renew",
        )

    upwind, downwind = [], []
    for s in range(spaces - 1):
        for v in range(vels):
            ahead = (s * vels + v, (s + 1) * vels + v)
            back = (ahead[1], ahead[0])
            upwind.append(back if v < vels // 2 else ahead)
            downwind.append(ahead if v < vels // 2 else back)
    rising = [(s, s + 1) for s in range(spaces - 1)]
    falling = [(s + 1, s) for s in range(spaces - 1)]
    both = ("space", "vel")

    def others(part):
        if vels == 2:
            return lax.ppermute(part, "vel", [(0, 1), (1, 0)])
        return lax.psum(part, "vel") - part

    x = dist.reshape(own, local)
    part, up, down, mask = moments(scal, x, kinds, table)
    for turn in range(STEPS):
        last = turn == STEPS - 1
        upw = lax.ppermute(up, both, upwind)
        dn = lax.ppermute(down, both, downwind)
        totals = part + others(part)
        below = lax.ppermute(totals[:, own - 2 * cells :], "space", rising)
        above = lax.ppermute(totals[:, : 2 * cells], "space", falling)
        cell, face_in, sums = inside(scal, x, totals, mask, table)
        face_edge, part = outside(
            scal, cell, upw, dn, below, above, totals, mask, table, sums
        )
        out = renew(last)(
            scal, boundary, x, cell, face_in, face_edge, part, others(part), totals, kinds, mask,
            table,
        )
        if last:
            (x,) = out
        else:
            x, part, up, down = out
    return x.reshape(planes, across, height, local)


def solution(mesh):
    spaces, vels = mesh.shape["space"], mesh.shape["vel"]
    return jax.shard_map(
        functools.partial(on_device, spaces=spaces, vels=vels),
        mesh=mesh,
        in_specs=(P("space", None, None, "vel"), P(), P()),
        out_specs=P("space", None, None, "vel"),
        check_vma=False,
    )
```

time: 119 us -> 73.8 us (0.62)
  the two profiles are of different devices: /device:TPU:23 before, /device:TPU:18 now
where the time goes in v1:
time: 73.8 us; the launch traced here: 72.9 us
  Pallas kernels  31 us (42%)
  starting transfers between devices  23.2 us (31%)
  waiting for transfers between devices  14.5 us (20%)
  local copies, waits for them, and re-layouts  3.95 us (5%)
    pallas_call x2, Pallas kernels, on_device(): renew(last)  11.5 us
    pallas_call x2, Pallas kernels, on_device(): outside(scal, cell, upw, dn, below, above, totals, mask, table, sums)  8.62 us
    pallas_call x2, Pallas kernels, on_device(): cell, face_in, sums = inside(scal, x, totals, mask, table)  8.16 us
    ppermute x4, waiting for transfers between devices, others(): return lax.ppermute(part, 'vel', [(0, 1), (1, 0)])  6.78 us
    ppermute x4, starting transfers between devices, others(): return lax.ppermute(part, 'vel', [(0, 1), (1, 0)])  5.44 us
    ppermute x2, starting transfers between devices, on_device(): dn = lax.ppermute(down, both, downwind)  5.17 us
    ppermute x2, waiting for transfers between devices, on_device(): above = lax.ppermute(totals[:, :2 * cells], 'space', falling)  4.94 us
    ppermute x2, starting transfers between devices, on_device(): above = lax.ppermute(totals[:, :2 * cells], 'space', falling)  4.73 us
  transfers between devices with their start and end apart: 12, of which 6 were waited for; matrix products, arithmetic and copies ran while one was open for 0% of the time, Pallas kernels for 11%

profile of v1, /device:TPU:18, one launch (start us, length us, event | category | flops | bytes accessed | tf_op | source)
XLA Modules:
  0.0 72.9 jit_solution(1682630622655267694)
XLA Ops:
  0.0 0.8 %pad_dynamic-slice_fusion = s32[8,8,8]{0,2,1:T(8,128)S(1)} fusion(s32[]{:T(128)S(6)} %select_n.16, s32[64,8,8]{0,2,1:T(8,128)} %param.5), kind=kLoop, calls=%fused_computation | loop fusion | bytes 18436 | tf_op jit(solution)/shard_map/dynamic_slice | solution.py:628
  0.8 0.1 copy.5
  0.9 0.1 reshape.10.kind_ref
  1.0 0.1 stack.39.scal_ref
  1.1 0.0 copy-start
  1.1 1.6 %copy-done = f32[4,8,8,2048]{3,2,1,0:T(8,128)S(1)} copy-done((f32[4,8,8,2048]{3,2,1,0:T(8,128)S(1)}, f32[4,8,8,2048]{3,2,1,0:T(8,128)}, u32[]{:S(2)}) %copy-start) | copy-done | bytes 2097176
  2.7 0.0 copy-start.3
  2.7 1.2 %copy-done.3 = bf16[128,4096]{1,0:T(8,128)(2,1)S(1)} copy-done((bf16[128,4096]{1,0:T(8,128)(2,1)S(1)}, bf16[128,4096]{1,0:T(8,128)(2,1)}, u32[]{:S(2)}) %copy-start.3) | copy-done | bytes 1048600
  3.9 2.7 %moments.1 = (f32[16,256]{1,0:T(8,128)S(1)}, f32[112,2048]{1,0:T(8,128)S(1)}, f32[48,2048]{1,0:T(8,128)S(1)}, f32[512,128]{1,0:T(8,128)S(1)}) custom-call(s32[7]{0:T(128)S(1)} %stack.39.scal_ref, f32[256,2048]{1,0:T(8,128)S(1)} %bitcast.9, s32[1,512]{1,0:T(1,128)S(1)} %reshape.10.kind_ref, bf16[128,4096]{1,0:T(8,128)(2,1)S(1)} %copy-done.3), custom_call_target="tpu_custom_call" | custom-call | flops 2000000000 | bytes 1048576 | tf_op jit(solution)/shard_map/moments/pallas_call | solution.py:729
  6.7 1.9 %collective-permute-start.1 = (f32[112,2048]{1,0:T(8,128)S(1)}, f32[112,2048]{1,0:T(8,128)S(1)}, u32[]{:S(2)}, u32[]{:S(2)}) collective-permute-start(f32[112,2048]{1,0:T(8,128)S(1)} %get-tuple-element.27), channel_id=1, source_target_pairs={{2,0},{1,3},{4,2},{3,5},{6,4},{5,7},{8,6},{7,9},{10,8},{9,11},{12,... | collective-permute-start | bytes 2752520 | tf_op jit(solution)/shard_map/ppermute | solution.py:732
  8.6 1.6 %collective-permute-start = (f32[16,256]{1,0:T(8,128)S(1)}, f32[16,256]{1,0:T(8,128)S(1)}, u32[]{:S(2)}, u32[]{:S(2)}) collective-permute-start(f32[16,256]{1,0:T(8,128)S(1)} %get-tuple-element.23), channel_id=1, source_target_pairs={{0,1},{1,0},{2,3},{3,2},{4,5},{5,4},{6,7},{7,6},{8,9},{9,8},{10,11... | collective-permute-start | bytes 49160 | tf_op jit(solution)/shard_map/ppermute | solution.py:725
  10.2 3.3 %collective-permute-start.2 = (f32[48,2048]{1,0:T(8,128)S(1)}, f32[48,2048]{1,0:T(8,128)S(1)}, u32[]{:S(2)}, u32[]{:S(2)}) collective-permute-start(f32[48,2048]{1,0:T(8,128)S(1)} %get-tuple-element.28), channel_id=1, source_target_pairs={{0,2},{3,1},{2,4},{5,3},{4,6},{7,5},{6,8},{9,7},{8,10},{11,9},{10,... | collective-permute-start | bytes 1179656 | tf_op jit(solution)/shard_map/ppermute | solution.py:733
  13.5 0.0 collective-permute-done
  13.5 2.3 %collective-permute-start.4 = (f32[16,128]{1,0:T(8,128)S(1)}, f32[16,128]{1,0:T(8,128)S(1)}, u32[]{:S(2)}, u32[]{:S(2)}) collective-permute-start(f32[16,128]{1,0:T(8,128)S(1)} %get-tuple-element.43), channel_id=1, source_target_pairs={{2,0},{4,2},{6,4},{8,6},{10,8},{12,10},{14,12},{16,14},{18,16},{20... | collective-permute-start | bytes 24584 | tf_op jit(solution)/shard_map/ppermute | solution.py:736
  15.8 2.0 %collective-permute-start.3 = (f32[16,128]{1,0:T(8,128)S(1)}, f32[16,128]{1,0:T(8,128)S(1)}, u32[]{:S(2)}, u32[]{:S(2)}) collective-permute-start(f32[16,128]{1,0:T(8,128)S(1)} %get-tuple-element.44), channel_id=1, source_target_pairs={{0,2},{2,4},{4,6},{6,8},{8,10},{10,12},{12,14},{14,16},{16,18},{18... | collective-permute-start | bytes 24584 | tf_op jit(solution)/shard_map/ppermute | solution.py:735
  17.8 0.0 copy-start.4
  17.9 4.1 %facesin.2 = (f32[256,2048]{1,0:T(8,128)S(1)}, f32[320,2048]{1,0:T(8,128)S(1)}, f32[320,128]{1,0:T(8,128)S(1)}) custom-call(s32[7]{0:T(128)S(1)} %stack.39.scal_ref, f32[256,2048]{1,0:T(8,128)S(1)} %bitcast.10, f32[16,256]{1,0:T(8,128)S(1)} %add.20.tot_ref, f32[512,128]{1,0:T(8,128)S(1)} %get-tuple-element.24.mask_ref, bf16[128,4096]{1,0:T(8,128)(2,1)S(1)} %copy-done.3), custom_call_target="tpu_custom_call" | custom-call | flops 6000000000 | bytes 1048576 | tf_op jit(solution)/shard_map/facesin/pallas_call | solution.py:737
  21.9 2.0 %collective-permute-done.4.above_ref = f32[16,128]{1,0:T(8,128)S(1)} collective-permute-done((f32[16,128]{1,0:T(8,128)S(1)}, f32[16,128]{1,0:T(8,128)S(1)}, u32[]{:S(2)}, u32[]{:S(2)}) %collective-permute-start.4) | collective-permute-done | bytes 8224 | tf_op jit(solution)/shard_map/ppermute | solution.py:736
  23.9 2.8 %collective-permute-done.3.below_ref = f32[16,128]{1,0:T(8,128)S(1)} collective-permute-done((f32[16,128]{1,0:T(8,128)S(1)}, f32[16,128]{1,0:T(8,128)S(1)}, u32[]{:S(2)}, u32[]{:S(2)}) %collective-permute-start.3) | collective-permute-done | bytes 8224 | tf_op jit(solution)/shard_map/ppermute | solution.py:735
  26.7 0.0 collective-permute-done.2.dn_ref
  26.7 0.0 collective-permute-done.1.upw_ref
  26.7 0.0 copy-done.4
  26.7 0.0 copy-start.1
  26.7 0.0 copy-start.2
  26.7 4.3 %faceb.2 = (f32[368,2048]{1,0:T(8,128)S(1)}, f32[16,768]{1,0:T(8,128)S(1)}) custom-call(s32[7]{0:T(128)S(1)} %stack.39.scal_ref, f32[256,2048]{1,0:T(8,128)S(1)} %get-tuple-element.25.cell_ref, f32[112,2048]{1,0:T(8,128)S(1)} %collective-permute-done.1.upw_ref, f32[48,2048]{1,0:T(8,128)S(1)} %collective-permute-done.2.dn_ref, ...), custom_call_target="tpu_custom_call" | custom-call | flops 6000000000 | bytes 1048576 | tf_op jit(solution)/shard_map/faceb/pallas_call | solution.py:738
  31.0 0.7 collective-permute-start.5
  31.7 3.5 %collective-permute-done.5.peer_ref = f32[16,768]{1,0:T(8,128)S(1)} collective-permute-done((f32[16,768]{1,0:T(8,128)S(1)}, f32[16,768]{1,0:T(8,128)S(1)}, u32[]{:S(2)}, u32[]{:S(2)}) %collective-permute-start.5) | collective-permute-done | bytes 49184 | tf_op jit(solution)/shard_map/ppermute | solution.py:725
  35.2 0.0 copy-done.1
  35.2 0.0 copy-done.2
  35.2 5.7 %renew.2 = (f32[256,2048]{1,0:T(8,128)S(1)}, f32[16,256]{1,0:T(8,128)S(1)}, f32[112,2048]{1,0:T(8,128)S(1)}, f32[48,2048]{1,0:T(8,128)S(1)}) custom-call(s32[7]{0:T(128)S(1)} %stack.39.scal_ref, f32[6]{0:T(128)S(1)} %copy-done.2, f32[256,2048]{1,0:T(8,128)S(1)} %bitcast.11, f32[256,2048]{1,0:T(8,128)S(1)} %get-tuple-element.25.cell_ref, ...), custom_call_target="tpu_custom_call" | custom-call | flops 6000000000 | bytes 1048576 | tf_op jit(solution)/shard_map/renew/pallas_call | solution.py:741
  40.9 1.9 %collective-permute-start.7 = (f32[112,2048]{1,0:T(8,128)S(1)}, f32[112,2048]{1,0:T(8,128)S(1)}, u32[]{:S(2)}, u32[]{:S(2)}) collective-permute-start(f32[112,2048]{1,0:T(8,128)S(1)} %get-tuple-element.36), channel_id=1, source_target_pairs={{2,0},{1,3},{4,2},{3,5},{6,4},{5,7},{8,6},{7,9},{10,8},{9,11},{12,... | collective-permute-start | bytes 2752520 | tf_op jit(solution)/shard_map/ppermute | solution.py:732
  42.8 0.7 collective-permute-start.6
  43.5 1.9 %collective-permute-start.8 = (f32[48,2048]{1,0:T(8,128)S(1)}, f32[48,2048]{1,0:T(8,128)S(1)}, u32[]{:S(2)}, u32[]{:S(2)}) collective-permute-start(f32[48,2048]{1,0:T(8,128)S(1)} %get-tuple-element.37), channel_id=1, source_target_pairs={{0,2},{3,1},{2,4},{5,3},{4,6},{7,5},{6,8},{9,7},{8,10},{11,9},{10,... | collective-permute-start | bytes 1179656 | tf_op jit(solution)/shard_map/ppermute | solution.py:733
  45.4 1.2 %collective-permute-done.6 = f32[16,256]{1,0:T(8,128)S(1)} collective-permute-done((f32[16,256]{1,0:T(8,128)S(1)}, f32[16,256]{1,0:T(8,128)S(1)}, u32[]{:S(2)}, u32[]{:S(2)}) %collective-permute-start.6) | collective-permute-done | bytes 16416 | tf_op jit(solution)/shard_map/ppermute | solution.py:725
  46.6 2.4 %collective-permute-start.10 = (f32[16,128]{1,0:T(8,128)S(1)}, f32[16,128]{1,0:T(8,128)S(1)}, u32[]{:S(2)}, u32[]{:S(2)}) collective-permute-start(f32[16,128]{1,0:T(8,128)S(1)} %get-tuple-element.41), channel_id=1, source_target_pairs={{2,0},{4,2},{6,4},{8,6},{10,8},{12,10},{14,12},{16,14},{18,16},{20... | collective-permute-start | bytes 24584 | tf_op jit(solution)/shard_map/ppermute | solution.py:736
  49.1 1.9 %collective-permute-start.9 = (f32[16,128]{1,0:T(8,128)S(1)}, f32[16,128]{1,0:T(8,128)S(1)}, u32[]{:S(2)}, u32[]{:S(2)}) collective-permute-start(f32[16,128]{1,0:T(8,128)S(1)} %get-tuple-element.42), channel_id=1, source_target_pairs={{0,2},{2,4},{4,6},{6,8},{8,10},{10,12},{12,14},{14,16},{16,18},{18... | collective-permute-start | bytes 24584 | tf_op jit(solution)/shard_map/ppermute | solution.py:735
  51.0 4.1 %facesin.3 = (f32[256,2048]{1,0:T(8,128)S(1)}, f32[320,2048]{1,0:T(8,128)S(1)}, f32[320,128]{1,0:T(8,128)S(1)}) custom-call(s32[7]{0:T(128)S(1)} %stack.39.scal_ref, f32[256,2048]{1,0:T(8,128)S(1)} %get-tuple-element.32.x_ref, f32[16,256]{1,0:T(8,128)S(1)} %add.21.tot_ref, f32[512,128]{1,0:T(8,128)S(1)} %get-tuple-element.24.mask_ref, ...), custom_call_target="tpu_custom_call" | custom-call | flops 6000000000 | bytes 1048576 | tf_op jit(solution)/shard_map/facesin/pallas_call | solution.py:737
  55.1 3.0 %collective-permute-done.10.above_ref = f32[16,128]{1,0:T(8,128)S(1)} collective-permute-done((f32[16,128]{1,0:T(8,128)S(1)}, f32[16,128]{1,0:T(8,128)S(1)}, u32[]{:S(2)}, u32[]{:S(2)}) %collective-permute-start.10) | collective-permute-done | bytes 8224 | tf_op jit(solution)/shard_map/ppermute | solution.py:736
  58.1 0.0 collective-permute-done.9.below_ref
  58.1 0.0 collective-permute-done.8.dn_ref
  58.1 0.0 collective-permute-done.7.upw_ref
  58.1 4.3 %faceb.3 = (f32[368,2048]{1,0:T(8,128)S(1)}, f32[16,768]{1,0:T(8,128)S(1)}) custom-call(s32[7]{0:T(128)S(1)} %stack.39.scal_ref, f32[256,2048]{1,0:T(8,128)S(1)} %get-tuple-element.34.cell_ref, f32[112,2048]{1,0:T(8,128)S(1)} %collective-permute-done.7.upw_ref, f32[48,2048]{1,0:T(8,128)S(1)} %collective-permute-done.8.dn_ref, ...), custom_call_target="tpu_custom_call" | custom-call | flops 6000000000 | bytes 1048576 | tf_op jit(solution)/shard_map/faceb/pallas_call | solution.py:738
  62.4 2.5 %collective-permute-start.11 = (f32[16,768]{1,0:T(8,128)S(1)}, f32[16,768]{1,0:T(8,128)S(1)}, u32[]{:S(2)}, u32[]{:S(2)}) collective-permute-start(f32[16,768]{1,0:T(8,128)S(1)} %get-tuple-element.40.mom_ref), channel_id=1, source_target_pairs={{0,1},{1,0},{2,3},{3,2},{4,5},{5,4},{6,7},{7,6},{8,9},{9,8},{10,11... | collective-permute-start | bytes 147464 | tf_op jit(solution)/shard_map/ppermute | solution.py:725
  65.0 2.1 %collective-permute-done.11.peer_ref = f32[16,768]{1,0:T(8,128)S(1)} collective-permute-done((f32[16,768]{1,0:T(8,128)S(1)}, f32[16,768]{1,0:T(8,128)S(1)}, u32[]{:S(2)}, u32[]{:S(2)}) %collective-permute-start.11) | collective-permute-done | bytes 49184 | tf_op jit(solution)/shard_map/ppermute | solution.py:725
  67.0 5.8 %renew.3 = f32[256,2048]{1,0:T(8,128)} custom-call(s32[7]{0:T(128)S(1)} %stack.39.scal_ref, f32[6]{0:T(128)S(1)} %copy-done.2, f32[256,2048]{1,0:T(8,128)S(1)} %get-tuple-element.32.x_ref, f32[256,2048]{1,0:T(8,128)S(1)} %get-tuple-element.34.cell_ref, f32[320,2048]{1,0:T(8,128)S(1)} %get-tuple-element.35.in_ref, ...), custom_call_target="tpu_custom_call" | custom-call | flops 6000000000 | bytes 1048576 | tf_op jit(solution)/shard_map/renew/pallas_call | solution.py:741
  (4 shorter events, 0.0 us)
Async XLA Ops:
  1.1 1.6 %copy-start = (f32[4,8,8,2048]{3,2,1,0:T(8,128)S(1)}, f32[4,8,8,2048]{3,2,1,0:T(8,128)}, u32[]{:S(2)}) copy-start(f32[4,8,8,2048]{3,2,1,0:T(8,128)} %param.4) | copy-start | bytes 6291460
  2.7 1.2 %copy-start.3 = (bf16[128,4096]{1,0:T(8,128)(2,1)S(1)}, bf16[128,4096]{1,0:T(8,128)(2,1)}, u32[]{:S(2)}) copy-start(bf16[128,4096]{1,0:T(8,128)(2,1)} %constant.28.clone.table_ref) | copy-start | bytes 3145732
  6.7 20.0 %collective-permute-start.1 = (f32[112,2048]{1,0:T(8,128)S(1)}, f32[112,2048]{1,0:T(8,128)S(1)}, u32[]{:S(2)}, u32[]{:S(2)}) collective-permute-start(f32[112,2048]{1,0:T(8,128)S(1)} %get-tuple-element.27), channel_id=1, source_target_pairs={{2,0},{1,3},{4,2},{3,5},{6,4},{5,7},{8,6},{7,9},{10,8},{9,11},{12,... | collective-permute-start | bytes 2752520 | tf_op jit(solution)/shard_map/ppermute | solution.py:732
  8.6 4.9 %collective-permute-start = (f32[16,256]{1,0:T(8,128)S(1)}, f32[16,256]{1,0:T(8,128)S(1)}, u32[]{:S(2)}, u32[]{:S(2)}) collective-permute-start(f32[16,256]{1,0:T(8,128)S(1)} %get-tuple-element.23), channel_id=1, source_target_pairs={{0,1},{1,0},{2,3},{3,2},{4,5},{5,4},{6,7},{7,6},{8,9},{9,8},{10,11... | collective-permute-start | bytes 49160 | tf_op jit(solution)/shard_map/ppermute | solution.py:725
  10.2 16.5 %collective-permute-start.2 = (f32[48,2048]{1,0:T(8,128)S(1)}, f32[48,2048]{1,0:T(8,128)S(1)}, u32[]{:S(2)}, u32[]{:S(2)}) collective-permute-start(f32[48,2048]{1,0:T(8,128)S(1)} %get-tuple-element.28), channel_id=1, source_target_pairs={{0,2},{3,1},{2,4},{5,3},{4,6},{7,5},{6,8},{9,7},{8,10},{11,9},{10,... | collective-permute-start | bytes 1179656 | tf_op jit(solution)/shard_map/ppermute | solution.py:733
  13.5 10.4 %collective-permute-start.4 = (f32[16,128]{1,0:T(8,128)S(1)}, f32[16,128]{1,0:T(8,128)S(1)}, u32[]{:S(2)}, u32[]{:S(2)}) collective-permute-start(f32[16,128]{1,0:T(8,128)S(1)} %get-tuple-element.43), channel_id=1, source_target_pairs={{2,0},{4,2},{6,4},{8,6},{10,8},{12,10},{14,12},{16,14},{18,16},{20... | collective-permute-start | bytes 24584 | tf_op jit(solution)/shard_map/ppermute | solution.py:736
  15.8 10.9 %collective-permute-start.3 = (f32[16,128]{1,0:T(8,128)S(1)}, f32[16,128]{1,0:T(8,128)S(1)}, u32[]{:S(2)}, u32[]{:S(2)}) collective-permute-start(f32[16,128]{1,0:T(8,128)S(1)} %get-tuple-element.44), channel_id=1, source_target_pairs={{0,2},{2,4},{4,6},{6,8},{8,10},{10,12},{12,14},{14,16},{16,18},{18... | collective-permute-start | bytes 24584 | tf_op jit(solution)/shard_map/ppermute | solution.py:735
  17.8 8.9 %copy-start.4 = (bf16[128,4096]{1,0:T(8,128)(2,1)S(1)}, bf16[128,4096]{1,0:T(8,128)(2,1)}, u32[]{:S(2)}) copy-start(bf16[128,4096]{1,0:T(8,128)(2,1)} %constant.28.clone.table_ref) | copy-start | bytes 3145732
  26.7 8.5 %copy-start.1 = (f32[4,8,8,2048]{3,2,1,0:T(8,128)S(1)}, f32[4,8,8,2048]{3,2,1,0:T(8,128)}, u32[]{:S(2)}) copy-start(f32[4,8,8,2048]{3,2,1,0:T(8,128)} %param.4) | copy-start | bytes 6291460
  26.7 8.5 %copy-start.2 = (f32[6]{0:T(128)S(1)}, f32[6]{0:T(128)}, u32[]{:S(2)}) copy-start(f32[6]{0:T(128)} %bound_ref.3) | copy-start | bytes 76
  31.0 4.1 %collective-permute-start.5 = (f32[16,768]{1,0:T(8,128)S(1)}, f32[16,768]{1,0:T(8,128)S(1)}, u32[]{:S(2)}, u32[]{:S(2)}) collective-permute-start(f32[16,768]{1,0:T(8,128)S(1)} %get-tuple-element.31.mom_ref), channel_id=1, source_target_pairs={{0,1},{1,0},{2,3},{3,2},{4,5},{5,4},{6,7},{7,6},{8,9},{9,8},{10,11... | collective-permute-start | bytes 147464 | tf_op jit(solution)/shard_map/ppermute | solution.py:725
  40.9 17.2 %collective-permute-start.7 = (f32[112,2048]{1,0:T(8,128)S(1)}, f32[112,2048]{1,0:T(8,128)S(1)}, u32[]{:S(2)}, u32[]{:S(2)}) collective-permute-start(f32[112,2048]{1,0:T(8,128)S(1)} %get-tuple-element.36), channel_id=1, source_target_pairs={{2,0},{1,3},{4,2},{3,5},{6,4},{5,7},{8,6},{7,9},{10,8},{9,11},{12,... | collective-permute-start | bytes 2752520 | tf_op jit(solution)/shard_map/ppermute | solution.py:732
  42.8 3.8 %collective-permute-start.6 = (f32[16,256]{1,0:T(8,128)S(1)}, f32[16,256]{1,0:T(8,128)S(1)}, u32[]{:S(2)}, u32[]{:S(2)}) collective-permute-start(f32[16,256]{1,0:T(8,128)S(1)} %get-tuple-element.33), channel_id=1, source_target_pairs={{0,1},{1,0},{2,3},{3,2},{4,5},{5,4},{6,7},{7,6},{8,9},{9,8},{10,11... | collective-permute-start | bytes 49160 | tf_op jit(solution)/shard_map/ppermute | solution.py:725
  43.5 14.6 %collective-permute-start.8 = (f32[48,2048]{1,0:T(8,128)S(1)}, f32[48,2048]{1,0:T(8,128)S(1)}, u32[]{:S(2)}, u32[]{:S(2)}) collective-permute-start(f32[48,2048]{1,0:T(8,128)S(1)} %get-tuple-element.37), channel_id=1, source_target_pairs={{0,2},{3,1},{2,4},{5,3},{4,6},{7,5},{6,8},{9,7},{8,10},{11,9},{10,... | collective-permute-start | bytes 1179656 | tf_op jit(solution)/shard_map/ppermute | solution.py:733
  46.6 11.5 %collective-permute-start.10 = (f32[16,128]{1,0:T(8,128)S(1)}, f32[16,128]{1,0:T(8,128)S(1)}, u32[]{:S(2)}, u32[]{:S(2)}) collective-permute-start(f32[16,128]{1,0:T(8,128)S(1)} %get-tuple-element.41), channel_id=1, source_target_pairs={{2,0},{4,2},{6,4},{8,6},{10,8},{12,10},{14,12},{16,14},{18,16},{20... | collective-permute-start | bytes 24584 | tf_op jit(solution)/shard_map/ppermute | solution.py:736
  49.1 9.0 %collective-permute-start.9 = (f32[16,128]{1,0:T(8,128)S(1)}, f32[16,128]{1,0:T(8,128)S(1)}, u32[]{:S(2)}, u32[]{:S(2)}) collective-permute-start(f32[16,128]{1,0:T(8,128)S(1)} %get-tuple-element.42), channel_id=1, source_target_pairs={{0,2},{2,4},{4,6},{6,8},{8,10},{10,12},{12,14},{14,16},{16,18},{18... | collective-permute-start | bytes 24584 | tf_op jit(solution)/shard_map/ppermute | solution.py:735
  62.4 4.6 %collective-permute-start.11 = (f32[16,768]{1,0:T(8,128)S(1)}, f32[16,768]{1,0:T(8,128)S(1)}, u32[]{:S(2)}, u32[]{:S(2)}) collective-permute-start(f32[16,768]{1,0:T(8,128)S(1)} %get-tuple-element.40.mom_ref), channel_id=1, source_target_pairs={{0,1},{1,0},{2,3},{3,2},{4,5},{5,4},{6,7},{7,6},{8,9},{9,8},{10,11... | collective-permute-start | bytes 147464 | tf_op jit(solution)/shard_map/ppermute | solution.py:725

commit v2 on v1

--- a/solution.py
+++ b/solution.py
@@ -25,6 +25,7 @@
 TILE = NODES * NODES
 ROWS = 8
 HALFTILE = 128
+KEYS = 64
 VMEM_LIMIT = 24 * 2**20
 
 
@@ -38,7 +39,7 @@
     low = [v - h for v, h in zip(third, high)]
     base = [np.ones_like(n), *m, m[0] * m[0], m[1] * m[1], m[2] * m[2]]
     base += [m[0] * m[1], m[0] * m[2], m[1] * m[2], *high, *low]
-    table = np.zeros((HALFTILE, NODES**3), np.float32)
+    table = np.zeros((KEYS, NODES**3), np.float32)
     for part in range(3):
         table[part * COLS : (part + 1) * COLS] = np.stack(base)
     return jnp.asarray(table, jnp.bfloat16)
@@ -96,9 +97,8 @@
     g = -0.5 * LOG2E / temper
     speed_sq = velocity[0] * velocity[0] + velocity[1] * velocity[1] + velocity[2] * velocity[2]
     square = g * (UNIT * UNIT)
-    zero = jnp.zeros_like(g)
     linear = [(-2.0 * UNIT) * g * velocity[e] for e in range(3)]
-    return [g * speed_sq, *linear, square, square, square] + [zero] * 9
+    return [g * speed_sq, *linear, square, square, square]
 
 
 def shakhov_coefs(amplitude, density, velocity, temper, heat):
@@ -125,16 +125,20 @@
 
 
 def transposed_parts(coefs, extras, work):
-    work[...] = jnp.zeros(work.shape, jnp.float32)
+    count = work.shape[1]
+    work[0:COLS, :] = jnp.zeros((COLS, count), jnp.float32)
+    work[3 * COLS :, :] = jnp.zeros((KEYS - 3 * COLS, count), jnp.float32)
     for row, value in enumerate(coefs):
-        high = value.astype(jnp.bfloat16).astype(jnp.float32)
-        rest = value - high
-        middle = rest.astype(jnp.bfloat16).astype(jnp.float32)
-        work[row : row + 1, :] = high
-        work[COLS + row : COLS + row + 1, :] = middle
-        work[2 * COLS + row : 2 * COLS + row + 1, :] = rest - middle
+        work[row : row + 1, :] = value
     for row, value in enumerate(extras):
         work[3 * COLS + row : 3 * COLS + row + 1, :] = value
+    value = work[0:COLS, :]
+    high = value.astype(jnp.bfloat16).astype(jnp.float32)
+    rest = value - high
+    middle = rest.astype(jnp.bfloat16).astype(jnp.float32)
+    work[0:COLS, :] = high
+    work[COLS : 2 * COLS, :] = middle
+    work[2 * COLS : 3 * COLS, :] = rest - middle
     return jnp.transpose(work[...], (1, 0))
 
 
@@ -159,21 +163,37 @@
 
 
 def add_sends(scal_ref, x_ref, up_ref, down_ref, lanes):
-    inner = down_ref.shape[0]
-    far = pl.multiple_of(scal_ref[2], ROWS)
-    near = pl.multiple_of(scal_ref[3], ROWS)
-    down = pl.multiple_of(scal_ref[6], ROWS)
-    up_ref[:inner, lanes] = x_ref[pl.ds(far, inner), lanes]
-    up_ref[inner:, lanes] = x_ref[pl.ds(near, up_ref.shape[0] - inner), lanes]
-    down_ref[:, lanes] = x_ref[pl.ds(down, inner), lanes]
+    cells = ROWS * ROWS
+    short = down_ref.shape[0]
+
+    def pack(plane, ref):
+        ref[short - ROWS : short, lanes] = jnp.zeros((ROWS, TILE), jnp.float32)
+        for y in range(1, ROWS - 1):
+            column = x_ref[pl.ds(pl.multiple_of(plane * cells + y * ROWS, ROWS), ROWS), lanes]
+            first = (y - 1) * (ROWS - 2)
+            if y == 1:
+                ref[0:ROWS, lanes] = column
+            else:
+                ref[first + 1 : first + ROWS - 1, lanes] = column[1 : ROWS - 1]
+
+    pack(scal_ref[2], up_ref)
+    near = pl.multiple_of(scal_ref[3] * cells, ROWS)
+    up_ref[short:, lanes] = x_ref[pl.ds(near, cells), lanes]
+    pack(scal_ref[6], down_ref)
+
+
+def sends_kernel(scal_ref, x_ref, up_ref, down_ref):
+    @pl.loop(0, x_ref.shape[1] // TILE)
+    def _(n):
+        add_sends(scal_ref, x_ref, up_ref, down_ref, tile_lanes(n))
 
 
 def unroll_of(tiles):
-    return 2 if tiles % 2 == 0 else 1
+    return 8 if tiles % 8 == 0 else 4 if tiles % 4 == 0 else 2 if tiles % 2 == 0 else 1
 
 
 def moments_kernel(
-    scal_ref, x_ref, kind_ref, table_ref, out_ref, up_ref, down_ref, mask_ref, acc_ref, work_ref
+    scal_ref, x_ref, kind_ref, table_ref, out_ref, mask_ref, acc_ref, work_ref
 ):
     acc_ref[...] = jnp.zeros_like(acc_ref)
 
@@ -183,7 +203,6 @@
         high, low = split(x_ref[:, lanes])
         table = table_ref[:, tile_lanes(scal_ref[1] + n)]
         acc_ref[...] += dot_nt(high, table) + dot_nt(low, table)
-        add_sends(scal_ref, x_ref, up_ref, down_ref, lanes)
 
     out_ref[...] = WEIGHT * jnp.transpose(acc_ref[...], (1, 0))[:COLS]
     fluid = (kind_ref[...] == 1).astype(jnp.float32)
@@ -378,10 +397,13 @@
             kx, hx = x_factors(scal_ref, n)
             for r in range(0, ghosts, 16):
                 rows = slice(r, r + 16)
-                if r < inner + cells:
-                    f = upw_ref[rows, lanes]
+                short = dn_ref.shape[0]
+                if inner <= r < inner + cells:
+                    f = upw_ref[short + r - inner : short + r - inner + 16, lanes]
                 else:
-                    f = dn_ref[r - inner - cells : r - inner - cells + 16, lanes]
+                    ref, y = (upw_ref, r // ROWS) if r < inner else (dn_ref, (r - inner - cells) // ROWS)
+                    first = [(y + i) * (ROWS - 2) for i in range(2)]
+                    f = jnp.concatenate([ref[a : a + ROWS, lanes] for a in first], axis=0)
                 slab_ref[rows, k * TILE : (k + 1) * TILE] = twice(alpha_ref[rows, :]) * f + jnp.exp2(
                     res_ref[rows, :]
                 ) * res_ref[ghosts + r : ghosts + r + 16, :]
@@ -434,7 +456,7 @@
     face_z = face_y + planes * cells
     used = face_z + planes * inner
     if sum_ref.shape[0] > used:
-        sum_ref[used:, :] = jnp.zeros((sum_ref.shape[0] - used, HALFTILE), jnp.float32)
+        sum_ref[used:, :] = jnp.zeros((sum_ref.shape[0] - used, KEYS), jnp.float32)
 
     def place(row, size, source, at):
         sum_ref[pl.ds(pl.multiple_of(row, ROWS), size), :] = source[at : at + size, :]
@@ -616,11 +638,11 @@
         [
             neg,
             vel * tiles,
-            height + jnp.where(neg == 1, cells, own - 2 * cells),
-            jnp.where(neg == 1, 0, own - cells),
+            jnp.where(neg == 1, 1, planes - 2),
+            jnp.where(neg == 1, 0, planes - 1),
             (space > 0).astype(jnp.int32),
             (space < spaces - 1).astype(jnp.int32),
-            height + jnp.where(neg == 1, own - cells, 0),
+            jnp.where(neg == 1, planes - 1, 0),
         ]
     ).astype(jnp.int32)
     table = node_table()
@@ -637,14 +659,24 @@
     cost = lambda us: pl.CostEstimate(
         flops=int(us * 1e9), bytes_accessed=1 << 20, transcendentals=0
     )
-    sends = [shape(COLS, own), shape(inner + cells, local), shape(inner, local)]
-
+    short = -(-((across - 2) * (height - 2) + 2) // ROWS) * ROWS
+    sends = [shape(short + cells, local), shape(short, local)]
+
+    sender = pl.pallas_call(
+        sends_kernel,
+        in_specs=[smem, vmem],
+        out_specs=[vmem] * 2,
+        out_shape=sends,
+        compiler_params=params,
+        cost_estimate=cost(1),
+        name="sends",
+    )
     moments = pl.pallas_call(
         moments_kernel,
         in_specs=[smem] + [vmem] * 3,
-        out_specs=[vmem] * 4,
-        out_shape=sends + [shape(extended, HALFTILE)],
-        scratch_shapes=[scratch(own, HALFTILE), scratch(HALFTILE, extended)],
+        out_specs=[vmem] * 2,
+        out_shape=[shape(COLS, own), shape(extended, HALFTILE)],
+        scratch_shapes=[scratch(own, KEYS), scratch(KEYS, extended)],
         compiler_params=params,
         cost_estimate=cost(2),
         name="moments",
@@ -653,10 +685,10 @@
         functools.partial(inner_kernel, planes=planes),
         in_specs=[smem] + [vmem] * 4,
         out_specs=[vmem] * 3,
-        out_shape=[shape(own, local), shape(faces_in, local), shape(faces_in, HALFTILE)],
+        out_shape=[shape(own, local), shape(faces_in, local), shape(faces_in, KEYS)],
         scratch_shapes=[
-            scratch(HALFTILE, own),
-            packed(2 * own, HALFTILE),
+            scratch(KEYS, own),
+            packed(2 * own, KEYS),
             scratch(own, HALFTILE),
             packed(faces_in, 2 * TILE * unroll),
         ]
@@ -672,14 +704,14 @@
         out_shape=[shape(faces_edge, local), shape(COLS, padded)],
         scratch_shapes=[
             scratch(COLS, 4 * cells),
-            scratch(HALFTILE, 4 * cells),
-            scratch(4 * cells, HALFTILE),
-            packed(2 * ghosts, HALFTILE),
+            scratch(KEYS, 4 * cells),
+            scratch(4 * cells, KEYS),
+            packed(2 * ghosts, KEYS),
             scratch(ghosts, HALFTILE),
             scratch(ghosts, TILE * unroll),
             packed(faces_edge, 2 * TILE * unroll),
-            scratch(faces_edge, HALFTILE),
-            scratch(padded, HALFTILE),
+            scratch(faces_edge, KEYS),
+            scratch(padded, KEYS),
         ]
         + [scratch(2 * ghosts, TILE)] * unroll,
         compiler_params=params,
@@ -692,14 +724,14 @@
             functools.partial(renew_kernel, planes=planes, last=last, unroll=unroll),
             in_specs=[smem, smem] + [vmem] * 10,
             out_specs=[vmem] * (1 if last else 4),
-            out_shape=[shape(own, local)] + ([] if last else sends),
+            out_shape=[shape(own, local)] + ([] if last else [shape(COLS, own)] + sends),
             scratch_shapes=[
-                scratch(HALFTILE, own),
-                scratch(HALFTILE, padded),
-                packed(2 * faces + own, HALFTILE),
+                scratch(KEYS, own),
+                scratch(KEYS, padded),
+                packed(2 * faces + own, KEYS),
                 scratch(faces, HALFTILE),
                 scratch(own, HALFTILE),
-                scratch(own, HALFTILE),
+                scratch(own, KEYS),
                 packed(own, 2 * TILE * unroll),
             ]
             + [scratch(2 * faces + own, TILE)] * unroll
@@ -726,7 +758,8 @@
         return lax.psum(part, "vel") - part
 
     x = dist.reshape(own, local)
-    part, up, down, mask = moments(scal, x, kinds, table)
+    up, down = sender(scal, x)
+    part, mask = moments(scal, x, kinds, table)
     for turn in range(STEPS):
         last = turn == STEPS - 1
         upw = lax.ppermute(up, both, upwind)

time: 73.8 us -> 66.6 us (0.902)
  Pallas kernels: 31 us -> 26.5 us
  waiting for transfers between devices: 14.5 us -> 13.1 us
  local copies, waits for them, and re-layouts: 3.95 us -> 3 us
    ppermute x2, waiting for transfers between devices: 4.94 us -> 1.19 us  [on_device(): above = lax.ppermute(totals[:, :2 * cells], 'space', falling)]
    pallas_call x2, Pallas kernels: 8.16 us -> 5.77 us  [on_device(): cell, face_in, sums = inside(scal, x, totals, mask, table)]
    pallas_call x2, Pallas kernels: 8.62 us -> 6.72 us  [on_device(): outside(scal, cell, upw, dn, below, above, totals, mask, table, sums)]
    ppermute x2, starting transfers between devices: 5.17 us -> 7.05 us  [on_device(): dn = lax.ppermute(down, both, downwind)]
    pallas_call x2, Pallas kernels: 11.5 us -> 9.75 us  [on_device(): renew(last)]
    ppermute x4, starting transfers between devices: 5.44 us -> 3.74 us  [others(): return lax.ppermute(part, 'vel', [(0, 1), (1, 0)])]
    pallas_call x1 -> x2, Pallas kernels: 2.75 us -> 4.23 us  [the longest x1 2.55 us: on_device(): part, mask = moments(scal, x, kinds, table)]
    ppermute x2, waiting for transfers between devices: 2.81 us -> 4.29 us  [on_device(): below = lax.ppermute(totals[:, own - 2 * cells:], 'space', rising)]
  transfers between devices with their start and end apart: 12 -> 12, of which waited for: 6 -> 5; matrix products, arithmetic and copies ran while one was open for 0% -> 0% of each run, Pallas kernels for 11% -> 13%
where the time goes in v2:
time: 66.6 us; the launch traced here: 66.2 us
  Pallas kernels  26.5 us (40%)
  starting transfers between devices  23.4 us (35%)
  waiting for transfers between devices  13.1 us (20%)
  local copies, waits for them, and re-layouts  3 us (5%)
    pallas_call x2, Pallas kernels, on_device(): renew(last)  9.75 us
    ppermute x4, waiting for transfers between devices, others(): return lax.ppermute(part, 'vel', [(0, 1), (1, 0)])  7.56 us
    ppermute x2, starting transfers between devices, on_device(): dn = lax.ppermute(down, both, downwind)  7.05 us
    pallas_call x2, Pallas kernels, on_device(): outside(scal, cell, upw, dn, below, above, totals, mask, table, sums)  6.72 us
    pallas_call x2, Pallas kernels, on_device(): cell, face_in, sums = inside(scal, x, totals, mask, table)  5.77 us
    ppermute x2, starting transfers between devices, on_device(): below = lax.ppermute(totals[:, own - 2 * cells:], 'space', rising)  4.63 us
    ppermute x2, waiting for transfers between devices, on_device(): below = lax.ppermute(totals[:, own - 2 * cells:], 'space', rising)  4.29 us
    ppermute x2, starting transfers between devices, on_device(): above = lax.ppermute(totals[:, :2 * cells], 'space', falling)  4.2 us
  transfers between devices with their start and end apart: 12, of which 5 were waited for; matrix products, arithmetic and copies ran while one was open for 0% of the time, Pallas kernels for 13%

profile of v2, /device:TPU:18, one launch (start us, length us, event | category | flops | bytes accessed | tf_op | source)
XLA Modules:
  0.0 66.2 jit_solution(5100325106600691985)
XLA Ops:
  0.0 0.0 copy-start.5
  0.0 0.1 stack.39.scal_ref
  0.1 0.0 copy-start
  0.1 1.6 %copy-done = f32[4,8,8,2048]{3,2,1,0:T(8,128)S(1)} copy-done((f32[4,8,8,2048]{3,2,1,0:T(8,128)S(1)}, f32[4,8,8,2048]{3,2,1,0:T(8,128)}, u32[]{:S(2)}) %copy-start) | copy-done | bytes 2097176
  1.7 0.0 copy-start.1
  1.7 1.7 %sends.1 = (f32[104,2048]{1,0:T(8,128)}, f32[40,2048]{1,0:T(8,128)S(1)}) custom-call(s32[7]{0:T(128)S(1)} %stack.39.scal_ref, f32[256,2048]{1,0:T(8,128)S(1)} %bitcast.9), custom_call_target="tpu_custom_call" | custom-call | flops 1000000000 | bytes 1048576 | tf_op jit(solution)/shard_map/sends/pallas_call | solution.py:761
  3.4 1.9 %collective-permute-start.1 = (f32[104,2048]{1,0:T(8,128)}, f32[104,2048]{1,0:T(8,128)S(1)}, u32[]{:S(2)}, u32[]{:S(2)}) collective-permute-start(f32[104,2048]{1,0:T(8,128)} %get-tuple-element.27), channel_id=1, source_target_pairs={{2,0},{1,3},{4,2},{3,5},{6,4},{5,7},{8,6},{7,9},{10,8},{9,11},{12,... | collective-permute-start | bytes 2555912 | tf_op jit(solution)/shard_map/ppermute | solution.py:765
  5.3 0.0 copy-done.5
  5.3 0.1 pad_dynamic-slice_fusion
  5.4 0.1 copy.5
  5.5 0.1 reshape.10.kind_ref
  5.6 0.0 copy-done.1
  5.6 0.0 copy-start.3
  5.6 1.0 %copy-done.3 = bf16[64,4096]{1,0:T(8,128)(2,1)S(1)} copy-done((bf16[64,4096]{1,0:T(8,128)(2,1)S(1)}, bf16[64,4096]{1,0:T(8,128)(2,1)}, u32[]{:S(2)}) %copy-start.3) | copy-done | bytes 524312
  6.6 2.6 %moments.1 = (f32[16,256]{1,0:T(8,128)S(1)}, f32[512,128]{1,0:T(8,128)S(1)}) custom-call(s32[7]{0:T(128)S(1)} %stack.39.scal_ref, f32[256,2048]{1,0:T(8,128)S(1)} %bitcast.10, s32[1,512]{1,0:T(1,128)S(1)} %reshape.10.kind_ref, bf16[64,4096]{1,0:T(8,128)(2,1)S(1)} %copy-done.3), custom_call_target="tpu_custom_call" | custom-call | flops 2000000000 | bytes 1048576 | tf_op jit(solution)/shard_map/moments/pallas_call | solution.py:762
  9.2 1.6 %collective-permute-start = (f32[16,256]{1,0:T(8,128)S(1)}, f32[16,256]{1,0:T(8,128)S(1)}, u32[]{:S(2)}, u32[]{:S(2)}) collective-permute-start(f32[16,256]{1,0:T(8,128)S(1)} %get-tuple-element.23), channel_id=1, source_target_pairs={{0,1},{1,0},{2,3},{3,2},{4,5},{5,4},{6,7},{7,6},{8,9},{9,8},{10,11... | collective-permute-start | bytes 49160 | tf_op jit(solution)/shard_map/ppermute | solution.py:757
  10.8 3.3 %collective-permute-start.2 = (f32[40,2048]{1,0:T(8,128)S(1)}, f32[40,2048]{1,0:T(8,128)S(1)}, u32[]{:S(2)}, u32[]{:S(2)}) collective-permute-start(f32[40,2048]{1,0:T(8,128)S(1)} %get-tuple-element.28), channel_id=1, source_target_pairs={{0,2},{3,1},{2,4},{5,3},{4,6},{7,5},{6,8},{9,7},{8,10},{11,9},{10,... | collective-permute-start | bytes 983048 | tf_op jit(solution)/shard_map/ppermute | solution.py:766
  14.0 0.0 collective-permute-done
  14.1 2.3 %collective-permute-start.4 = (f32[16,128]{1,0:T(8,128)S(1)}, f32[16,128]{1,0:T(8,128)S(1)}, u32[]{:S(2)}, u32[]{:S(2)}) collective-permute-start(f32[16,128]{1,0:T(8,128)S(1)} %get-tuple-element.43), channel_id=1, source_target_pairs={{2,0},{4,2},{6,4},{8,6},{10,8},{12,10},{14,12},{16,14},{18,16},{20... | collective-permute-start | bytes 24584 | tf_op jit(solution)/shard_map/ppermute | solution.py:769
  16.4 2.0 %collective-permute-start.3 = (f32[16,128]{1,0:T(8,128)S(1)}, f32[16,128]{1,0:T(8,128)S(1)}, u32[]{:S(2)}, u32[]{:S(2)}) collective-permute-start(f32[16,128]{1,0:T(8,128)S(1)} %get-tuple-element.44), channel_id=1, source_target_pairs={{0,2},{2,4},{4,6},{6,8},{8,10},{10,12},{12,14},{14,16},{16,18},{18... | collective-permute-start | bytes 24584 | tf_op jit(solution)/shard_map/ppermute | solution.py:768
  18.4 0.0 copy-start.4
  18.4 2.9 %facesin.2 = (f32[256,2048]{1,0:T(8,128)S(1)}, f32[320,2048]{1,0:T(8,128)S(1)}, f32[320,64]{1,0:T(8,128)S(1)}) custom-call(s32[7]{0:T(128)S(1)} %stack.39.scal_ref, f32[256,2048]{1,0:T(8,128)S(1)} %bitcast.11, f32[16,256]{1,0:T(8,128)S(1)} %add.12.tot_ref, f32[512,128]{1,0:T(8,128)S(1)} %get-tuple-element.24.mask_ref, bf16[64,4096]{1,0:T(8,128)(2,1)S(1)} %copy-done.3), custom_call_target="tpu_custom_call" | custom-call | flops 6000000000 | bytes 1048576 | tf_op jit(solution)/shard_map/facesin/pallas_call | solution.py:770
  21.3 0.0 collective-permute-done.4.above_ref
  21.3 0.8 %collective-permute-done.3.below_ref = f32[16,128]{1,0:T(8,128)S(1)} collective-permute-done((f32[16,128]{1,0:T(8,128)S(1)}, f32[16,128]{1,0:T(8,128)S(1)}, u32[]{:S(2)}, u32[]{:S(2)}) %collective-permute-start.3) | collective-permute-done | bytes 8224 | tf_op jit(solution)/shard_map/ppermute | solution.py:768
  22.2 0.0 collective-permute-done.2.dn_ref
  22.2 0.0 collective-permute-done.1.upw_ref
  22.2 0.0 copy-done.4
  22.2 0.0 copy-start.2
  22.2 3.4 %faceb.2 = (f32[368,2048]{1,0:T(8,128)S(1)}, f32[16,768]{1,0:T(8,128)S(1)}) custom-call(s32[7]{0:T(128)S(1)} %stack.39.scal_ref, f32[256,2048]{1,0:T(8,128)S(1)} %get-tuple-element.25.cell_ref, f32[104,2048]{1,0:T(8,128)S(1)} %collective-permute-done.1.upw_ref, f32[40,2048]{1,0:T(8,128)S(1)} %collective-permute-done.2.dn_ref, ...), custom_call_target="tpu_custom_call" | custom-call | flops 6000000000 | bytes 1048576 | tf_op jit(solution)/shard_map/faceb/pallas_call | solution.py:771
  25.5 0.7 collective-permute-start.5
  26.2 3.5 %collective-permute-done.5.peer_ref = f32[16,768]{1,0:T(8,128)S(1)} collective-permute-done((f32[16,768]{1,0:T(8,128)S(1)}, f32[16,768]{1,0:T(8,128)S(1)}, u32[]{:S(2)}, u32[]{:S(2)}) %collective-permute-start.5) | collective-permute-done | bytes 49184 | tf_op jit(solution)/shard_map/ppermute | solution.py:757
  29.7 0.0 copy-done.2
  29.7 4.6 %renew.2 = (f32[256,2048]{1,0:T(8,128)S(1)}, f32[16,256]{1,0:T(8,128)S(1)}, f32[104,2048]{1,0:T(8,128)S(1)}, f32[40,2048]{1,0:T(8,128)S(1)}) custom-call(s32[7]{0:T(128)S(1)} %stack.39.scal_ref, f32[6]{0:T(128)S(1)} %copy-done.2, f32[256,2048]{1,0:T(8,128)S(1)} %bitcast.12, f32[256,2048]{1,0:T(8,128)S(1)} %get-tuple-element.25.cell_ref, ...), custom_call_target="tpu_custom_call" | custom-call | flops 6000000000 | bytes 1048576 | tf_op jit(solution)/shard_map/renew/pallas_call | solution.py:774
  34.3 1.9 %collective-permute-start.7 = (f32[104,2048]{1,0:T(8,128)S(1)}, f32[104,2048]{1,0:T(8,128)S(1)}, u32[]{:S(2)}, u32[]{:S(2)}) collective-permute-start(f32[104,2048]{1,0:T(8,128)S(1)} %get-tuple-element.36), channel_id=1, source_target_pairs={{2,0},{1,3},{4,2},{3,5},{6,4},{5,7},{8,6},{7,9},{10,8},{9,11},{12,... | collective-permute-start | bytes 2555912 | tf_op jit(solution)/shard_map/ppermute | solution.py:765
  36.2 1.4 %collective-permute-start.6 = (f32[16,256]{1,0:T(8,128)S(1)}, f32[16,256]{1,0:T(8,128)S(1)}, u32[]{:S(2)}, u32[]{:S(2)}) collective-permute-start(f32[16,256]{1,0:T(8,128)S(1)} %get-tuple-element.33), channel_id=1, source_target_pairs={{0,1},{1,0},{2,3},{3,2},{4,5},{5,4},{6,7},{7,6},{8,9},{9,8},{10,11... | collective-permute-start | bytes 49160 | tf_op jit(solution)/shard_map/ppermute | solution.py:757
  37.6 3.8 %collective-permute-start.8 = (f32[40,2048]{1,0:T(8,128)S(1)}, f32[40,2048]{1,0:T(8,128)S(1)}, u32[]{:S(2)}, u32[]{:S(2)}) collective-permute-start(f32[40,2048]{1,0:T(8,128)S(1)} %get-tuple-element.37), channel_id=1, source_target_pairs={{0,2},{3,1},{2,4},{5,3},{4,6},{7,5},{6,8},{9,7},{8,10},{11,9},{10,... | collective-permute-start | bytes 983048 | tf_op jit(solution)/shard_map/ppermute | solution.py:766
  41.4 0.0 collective-permute-done.6
  41.5 1.9 %collective-permute-start.10 = (f32[16,128]{1,0:T(8,128)S(1)}, f32[16,128]{1,0:T(8,128)S(1)}, u32[]{:S(2)}, u32[]{:S(2)}) collective-permute-start(f32[16,128]{1,0:T(8,128)S(1)} %get-tuple-element.41), channel_id=1, source_target_pairs={{2,0},{4,2},{6,4},{8,6},{10,8},{12,10},{14,12},{16,14},{18,16},{20... | collective-permute-start | bytes 24584 | tf_op jit(solution)/shard_map/ppermute | solution.py:769
  43.4 2.6 %collective-permute-start.9 = (f32[16,128]{1,0:T(8,128)S(1)}, f32[16,128]{1,0:T(8,128)S(1)}, u32[]{:S(2)}, u32[]{:S(2)}) collective-permute-start(f32[16,128]{1,0:T(8,128)S(1)} %get-tuple-element.42), channel_id=1, source_target_pairs={{0,2},{2,4},{4,6},{6,8},{8,10},{10,12},{12,14},{14,16},{16,18},{18... | collective-permute-start | bytes 24584 | tf_op jit(solution)/shard_map/ppermute | solution.py:768
  46.0 2.9 %facesin.3 = (f32[256,2048]{1,0:T(8,128)S(1)}, f32[320,2048]{1,0:T(8,128)S(1)}, f32[320,64]{1,0:T(8,128)S(1)}) custom-call(s32[7]{0:T(128)S(1)} %stack.39.scal_ref, f32[256,2048]{1,0:T(8,128)S(1)} %get-tuple-element.32.x_ref, f32[16,256]{1,0:T(8,128)S(1)} %add.13.tot_ref, f32[512,128]{1,0:T(8,128)S(1)} %get-tuple-element.24.mask_ref, ...), custom_call_target="tpu_custom_call" | custom-call | flops 6000000000 | bytes 1048576 | tf_op jit(solution)/shard_map/facesin/pallas_call | solution.py:770
  48.9 1.2 %collective-permute-done.10.above_ref = f32[16,128]{1,0:T(8,128)S(1)} collective-permute-done((f32[16,128]{1,0:T(8,128)S(1)}, f32[16,128]{1,0:T(8,128)S(1)}, u32[]{:S(2)}, u32[]{:S(2)}) %collective-permute-start.10) | collective-permute-done | bytes 8224 | tf_op jit(solution)/shard_map/ppermute | solution.py:769
  50.1 3.4 %collective-permute-done.9.below_ref = f32[16,128]{1,0:T(8,128)S(1)} collective-permute-done((f32[16,128]{1,0:T(8,128)S(1)}, f32[16,128]{1,0:T(8,128)S(1)}, u32[]{:S(2)}, u32[]{:S(2)}) %collective-permute-start.9) | collective-permute-done | bytes 8224 | tf_op jit(solution)/shard_map/ppermute | solution.py:768
  53.5 0.0 collective-permute-done.8.dn_ref
  53.5 0.0 collective-permute-done.7.upw_ref
  53.5 3.4 %faceb.3 = (f32[368,2048]{1,0:T(8,128)S(1)}, f32[16,768]{1,0:T(8,128)S(1)}) custom-call(s32[7]{0:T(128)S(1)} %stack.39.scal_ref, f32[256,2048]{1,0:T(8,128)S(1)} %get-tuple-element.34.cell_ref, f32[104,2048]{1,0:T(8,128)S(1)} %collective-permute-done.7.upw_ref, f32[40,2048]{1,0:T(8,128)S(1)} %collective-permute-done.8.dn_ref, ...), custom_call_target="tpu_custom_call" | custom-call | flops 6000000000 | bytes 1048576 | tf_op jit(solution)/shard_map/faceb/pallas_call | solution.py:771
  56.9 0.1 collective-permute-start.11
  57.0 4.1 %collective-permute-done.11.peer_ref = f32[16,768]{1,0:T(8,128)S(1)} collective-permute-done((f32[16,768]{1,0:T(8,128)S(1)}, f32[16,768]{1,0:T(8,128)S(1)}, u32[]{:S(2)}, u32[]{:S(2)}) %collective-permute-start.11) | collective-permute-done | bytes 49184 | tf_op jit(solution)/shard_map/ppermute | solution.py:757
  61.0 5.2 %renew.3 = f32[256,2048]{1,0:T(8,128)} custom-call(s32[7]{0:T(128)S(1)} %stack.39.scal_ref, f32[6]{0:T(128)S(1)} %copy-done.2, f32[256,2048]{1,0:T(8,128)S(1)} %get-tuple-element.32.x_ref, f32[256,2048]{1,0:T(8,128)S(1)} %get-tuple-element.34.cell_ref, f32[320,2048]{1,0:T(8,128)S(1)} %get-tuple-element.35.in_ref, ...), custom_call_target="tpu_custom_call" | custom-call | flops 6000000000 | bytes 1048576 | tf_op jit(solution)/shard_map/renew/pallas_call | solution.py:774
  (4 shorter events, 0.0 us)
Async XLA Ops:
  0.0 5.3 %copy-start.5 = (s32[64,8,8]{0,2,1:T(8,128)S(1)}, s32[64,8,8]{0,2,1:T(8,128)}, u32[]{:S(2)}) copy-start(s32[64,8,8]{0,2,1:T(8,128)} %param.5) | copy-start | bytes 49156
  0.1 1.6 %copy-start = (f32[4,8,8,2048]{3,2,1,0:T(8,128)S(1)}, f32[4,8,8,2048]{3,2,1,0:T(8,128)}, u32[]{:S(2)}) copy-start(f32[4,8,8,2048]{3,2,1,0:T(8,128)} %param.4) | copy-start | bytes 6291460
  1.7 3.9 %copy-start.1 = (f32[4,8,8,2048]{3,2,1,0:T(8,128)S(1)}, f32[4,8,8,2048]{3,2,1,0:T(8,128)}, u32[]{:S(2)}) copy-start(f32[4,8,8,2048]{3,2,1,0:T(8,128)} %param.4) | copy-start | bytes 6291460
  3.4 18.8 %collective-permute-start.1 = (f32[104,2048]{1,0:T(8,128)}, f32[104,2048]{1,0:T(8,128)S(1)}, u32[]{:S(2)}, u32[]{:S(2)}) collective-permute-start(f32[104,2048]{1,0:T(8,128)} %get-tuple-element.27), channel_id=1, source_target_pairs={{2,0},{1,3},{4,2},{3,5},{6,4},{5,7},{8,6},{7,9},{10,8},{9,11},{12,... | collective-permute-start | bytes 2555912 | tf_op jit(solution)/shard_map/ppermute | solution.py:765
  5.6 1.0 %copy-start.3 = (bf16[64,4096]{1,0:T(8,128)(2,1)S(1)}, bf16[64,4096]{1,0:T(8,128)(2,1)}, u32[]{:S(2)}) copy-start(bf16[64,4096]{1,0:T(8,128)(2,1)} %constant.26.clone.table_ref) | copy-start | bytes 1572868
  9.2 4.9 %collective-permute-start = (f32[16,256]{1,0:T(8,128)S(1)}, f32[16,256]{1,0:T(8,128)S(1)}, u32[]{:S(2)}, u32[]{:S(2)}) collective-permute-start(f32[16,256]{1,0:T(8,128)S(1)} %get-tuple-element.23), channel_id=1, source_target_pairs={{0,1},{1,0},{2,3},{3,2},{4,5},{5,4},{6,7},{7,6},{8,9},{9,8},{10,11... | collective-permute-start | bytes 49160 | tf_op jit(solution)/shard_map/ppermute | solution.py:757
  10.8 11.4 %collective-permute-start.2 = (f32[40,2048]{1,0:T(8,128)S(1)}, f32[40,2048]{1,0:T(8,128)S(1)}, u32[]{:S(2)}, u32[]{:S(2)}) collective-permute-start(f32[40,2048]{1,0:T(8,128)S(1)} %get-tuple-element.28), channel_id=1, source_target_pairs={{0,2},{3,1},{2,4},{5,3},{4,6},{7,5},{6,8},{9,7},{8,10},{11,9},{10,... | collective-permute-start | bytes 983048 | tf_op jit(solution)/shard_map/ppermute | solution.py:766
  14.1 7.3 %collective-permute-start.4 = (f32[16,128]{1,0:T(8,128)S(1)}, f32[16,128]{1,0:T(8,128)S(1)}, u32[]{:S(2)}, u32[]{:S(2)}) collective-permute-start(f32[16,128]{1,0:T(8,128)S(1)} %get-tuple-element.43), channel_id=1, source_target_pairs={{2,0},{4,2},{6,4},{8,6},{10,8},{12,10},{14,12},{16,14},{18,16},{20... | collective-permute-start | bytes 24584 | tf_op jit(solution)/shard_map/ppermute | solution.py:769
  16.4 5.8 %collective-permute-start.3 = (f32[16,128]{1,0:T(8,128)S(1)}, f32[16,128]{1,0:T(8,128)S(1)}, u32[]{:S(2)}, u32[]{:S(2)}) collective-permute-start(f32[16,128]{1,0:T(8,128)S(1)} %get-tuple-element.44), channel_id=1, source_target_pairs={{0,2},{2,4},{4,6},{6,8},{8,10},{10,12},{12,14},{14,16},{16,18},{18... | collective-permute-start | bytes 24584 | tf_op jit(solution)/shard_map/ppermute | solution.py:768
  18.4 3.8 %copy-start.4 = (bf16[64,4096]{1,0:T(8,128)(2,1)S(1)}, bf16[64,4096]{1,0:T(8,128)(2,1)}, u32[]{:S(2)}) copy-start(bf16[64,4096]{1,0:T(8,128)(2,1)} %constant.26.clone.table_ref) | copy-start | bytes 1572868
  22.2 7.5 %copy-start.2 = (f32[6]{0:T(128)S(1)}, f32[6]{0:T(128)}, u32[]{:S(2)}) copy-start(f32[6]{0:T(128)} %bound_ref.3) | copy-start | bytes 76
  25.5 4.1 %collective-permute-start.5 = (f32[16,768]{1,0:T(8,128)S(1)}, f32[16,768]{1,0:T(8,128)S(1)}, u32[]{:S(2)}, u32[]{:S(2)}) collective-permute-start(f32[16,768]{1,0:T(8,128)S(1)} %get-tuple-element.31.mom_ref), channel_id=1, source_target_pairs={{0,1},{1,0},{2,3},{3,2},{4,5},{5,4},{6,7},{7,6},{8,9},{9,8},{10,11... | collective-permute-start | bytes 147464 | tf_op jit(solution)/shard_map/ppermute | solution.py:757
  34.3 19.2 %collective-permute-start.7 = (f32[104,2048]{1,0:T(8,128)S(1)}, f32[104,2048]{1,0:T(8,128)S(1)}, u32[]{:S(2)}, u32[]{:S(2)}) collective-permute-start(f32[104,2048]{1,0:T(8,128)S(1)} %get-tuple-element.36), channel_id=1, source_target_pairs={{2,0},{1,3},{4,2},{3,5},{6,4},{5,7},{8,6},{7,9},{10,8},{9,11},{12,... | collective-permute-start | bytes 2555912 | tf_op jit(solution)/shard_map/ppermute | solution.py:765
  36.2 5.2 %collective-permute-start.6 = (f32[16,256]{1,0:T(8,128)S(1)}, f32[16,256]{1,0:T(8,128)S(1)}, u32[]{:S(2)}, u32[]{:S(2)}) collective-permute-start(f32[16,256]{1,0:T(8,128)S(1)} %get-tuple-element.33), channel_id=1, source_target_pairs={{0,1},{1,0},{2,3},{3,2},{4,5},{5,4},{6,7},{7,6},{8,9},{9,8},{10,11... | collective-permute-start | bytes 49160 | tf_op jit(solution)/shard_map/ppermute | solution.py:757
  37.6 15.9 %collective-permute-start.8 = (f32[40,2048]{1,0:T(8,128)S(1)}, f32[40,2048]{1,0:T(8,128)S(1)}, u32[]{:S(2)}, u32[]{:S(2)}) collective-permute-start(f32[40,2048]{1,0:T(8,128)S(1)} %get-tuple-element.37), channel_id=1, source_target_pairs={{0,2},{3,1},{2,4},{5,3},{4,6},{7,5},{6,8},{9,7},{8,10},{11,9},{10,... | collective-permute-start | bytes 983048 | tf_op jit(solution)/shard_map/ppermute | solution.py:766
  41.5 8.6 %collective-permute-start.10 = (f32[16,128]{1,0:T(8,128)S(1)}, f32[16,128]{1,0:T(8,128)S(1)}, u32[]{:S(2)}, u32[]{:S(2)}) collective-permute-start(f32[16,128]{1,0:T(8,128)S(1)} %get-tuple-element.41), channel_id=1, source_target_pairs={{2,0},{4,2},{6,4},{8,6},{10,8},{12,10},{14,12},{16,14},{18,16},{20... | collective-permute-start | bytes 24584 | tf_op jit(solution)/shard_map/ppermute | solution.py:769
  43.4 10.1 %collective-permute-start.9 = (f32[16,128]{1,0:T(8,128)S(1)}, f32[16,128]{1,0:T(8,128)S(1)}, u32[]{:S(2)}, u32[]{:S(2)}) collective-permute-start(f32[16,128]{1,0:T(8,128)S(1)} %get-tuple-element.42), channel_id=1, source_target_pairs={{0,2},{2,4},{4,6},{6,8},{8,10},{10,12},{12,14},{14,16},{16,18},{18... | collective-permute-start | bytes 24584 | tf_op jit(solution)/shard_map/ppermute | solution.py:768
  56.9 4.1 %collective-permute-start.11 = (f32[16,768]{1,0:T(8,128)S(1)}, f32[16,768]{1,0:T(8,128)S(1)}, u32[]{:S(2)}, u32[]{:S(2)}) collective-permute-start(f32[16,768]{1,0:T(8,128)S(1)} %get-tuple-element.40.mom_ref), channel_id=1, source_target_pairs={{0,1},{1,0},{2,3},{3,2},{4,5},{5,4},{6,7},{7,6},{8,9},{9,8},{10,11... | collective-permute-start | bytes 147464 | tf_op jit(solution)/shard_map/ppermute | solution.py:757

commit v3 on v2

--- a/solution.py
+++ b/solution.py
@@ -183,9 +183,8 @@
 
 
 def sends_kernel(scal_ref, x_ref, up_ref, down_ref):
-    @pl.loop(0, x_ref.shape[1] // TILE)
-    def _(n):
-        add_sends(scal_ref, x_ref, up_ref, down_ref, tile_lanes(n))
+    for n in range(x_ref.shape[1] // TILE):
+        add_sends(scal_ref, x_ref, up_ref, down_ref, slice(n * TILE, (n + 1) * TILE))
 
 
 def unroll_of(tiles):
@@ -196,11 +195,8 @@
     scal_ref, x_ref, kind_ref, table_ref, out_ref, mask_ref, acc_ref, work_ref
 ):
     acc_ref[...] = jnp.zeros_like(acc_ref)
-
-    @pl.loop(0, x_ref.shape[1] // TILE)
-    def _(n):
-        lanes = tile_lanes(n)
-        high, low = split(x_ref[:, lanes])
+    for n in range(x_ref.shape[1] // TILE):
+        high, low = split(x_ref[:, n * TILE : (n + 1) * TILE])
         table = table_ref[:, tile_lanes(scal_ref[1] + n)]
         acc_ref[...] += dot_nt(high, table) + dot_nt(low, table)
 
@@ -315,8 +311,6 @@
             table = table_ref[:, tile_lanes(scal_ref[1] + n)]
             tables.append(table)
             res_ref[...] = dot_nn(lhs_ref[...], table)
-        for k, res_ref in enumerate(res_refs):
-            n = m * unroll + k
             lanes = tile_lanes(n)
             kx, hx = x_factors(scal_ref, n)
             for r in range(0, own, 16):
@@ -391,8 +385,6 @@
             table = table_ref[:, tile_lanes(scal_ref[1] + n)]
             tables.append(table)
             res_ref[...] = dot_nn(lhs_ref[...], table)
-        for k, res_ref in enumerate(res_refs):
-            n = m * unroll + k
             lanes = tile_lanes(n)
             kx, hx = x_factors(scal_ref, n)
             for r in range(0, ghosts, 16):
@@ -562,8 +554,7 @@
             table = table_ref[:, tile_lanes(scal_ref[1] + n)]
             tables.append(table)
             res_ref[...] = dot_nn(lhs_ref[...], table)
-        for k, (res_ref, flux_ref) in enumerate(zip(res_refs, flux_refs)):
-            n = m * unroll + k
+            flux_ref = flux_refs[k]
             lanes = tile_lanes(n)
             digit = scal_ref[1] + n
             hx = (2 * digit + 1 - NODES).astype(jnp.float32) * (UNIT * DT)

time: 66.6 us -> 65.2 us (0.979)
  Pallas kernels: 26.5 us -> 25.2 us
    pallas_call x1, Pallas kernels: 2.55 us -> 1.41 us  [on_device(): part, mask = moments(scal, x, kinds, table)]
    ppermute x2, waiting for transfers between devices: 1.19 us -> 2.19 us  [on_device(): above = lax.ppermute(totals[:, :2 * cells], 'space', falling)]
  transfers between devices with their start and end apart: 12 -> 12, of which waited for: 5 -> 5; matrix products, arithmetic and copies ran while one was open for 0% -> 0% of each run, Pallas kernels for 13% -> 11%
where the time goes in v3:
time: 65.2 us; the launch traced here: 64.9 us
  Pallas kernels  25.2 us (39%)
  starting transfers between devices  22.9 us (35%)
  waiting for transfers between devices  13.5 us (21%)
  local copies, waits for them, and re-layouts  3 us (5%)
    pallas_call x2, Pallas kernels, on_device(): renew(last)  9.75 us
    ppermute x4, waiting for transfers between devices, others(): return lax.ppermute(part, 'vel', [(0, 1), (1, 0)])  7.03 us
    pallas_call x2, Pallas kernels, on_device(): outside(scal, cell, upw, dn, below, above, totals, mask, table, sums)  6.72 us
    ppermute x2, starting transfers between devices, on_device(): dn = lax.ppermute(down, both, downwind)  6.53 us
    pallas_call x2, Pallas kernels, on_device(): cell, face_in, sums = inside(scal, x, totals, mask, table)  5.78 us
    ppermute x2, starting transfers between devices, on_device(): above = lax.ppermute(totals[:, :2 * cells], 'space', falling)  4.57 us
    ppermute x2, waiting for transfers between devices, on_device(): below = lax.ppermute(totals[:, own - 2 * cells:], 'space', rising)  4.27 us
    ppermute x2, starting transfers between devices, on_device(): below = lax.ppermute(totals[:, own - 2 * cells:], 'space', rising)  4.26 us
  transfers between devices with their start and end apart: 12, of which 5 were waited for; matrix products, arithmetic and copies ran while one was open for 0% of the time, Pallas kernels for 11%

profile of v3, /device:TPU:18, one launch (start us, length us, event | category | flops | bytes accessed | tf_op | source)
XLA Modules:
  0.0 64.9 jit_solution(2396867040107648772)
XLA Ops:
  0.0 0.0 copy-start.5
  0.0 0.1 stack.39.scal_ref
  0.1 0.0 copy-start
  0.1 1.6 %copy-done = f32[4,8,8,2048]{3,2,1,0:T(8,128)S(1)} copy-done((f32[4,8,8,2048]{3,2,1,0:T(8,128)S(1)}, f32[4,8,8,2048]{3,2,1,0:T(8,128)}, u32[]{:S(2)}) %copy-start) | copy-done | bytes 2097176
  1.7 0.0 copy-start.1
  1.7 1.6 %sends.1 = (f32[104,2048]{1,0:T(8,128)}, f32[40,2048]{1,0:T(8,128)S(1)}) custom-call(s32[7]{0:T(128)S(1)} %stack.39.scal_ref, f32[256,2048]{1,0:T(8,128)S(1)} %bitcast.9), custom_call_target="tpu_custom_call" | custom-call | flops 1000000000 | bytes 1048576 | tf_op jit(solution)/shard_map/sends/pallas_call | solution.py:752
  3.2 1.9 %collective-permute-start.1 = (f32[104,2048]{1,0:T(8,128)}, f32[104,2048]{1,0:T(8,128)S(1)}, u32[]{:S(2)}, u32[]{:S(2)}) collective-permute-start(f32[104,2048]{1,0:T(8,128)} %get-tuple-element.27), channel_id=1, source_target_pairs={{2,0},{1,3},{4,2},{3,5},{6,4},{5,7},{8,6},{7,9},{10,8},{9,11},{12,... | collective-permute-start | bytes 2555912 | tf_op jit(solution)/shard_map/ppermute | solution.py:756
  5.2 0.0 copy-done.5
  5.2 0.1 pad_dynamic-slice_fusion
  5.3 0.1 copy.5
  5.3 0.1 reshape.10.kind_ref
  5.4 0.0 copy-done.1
  5.4 0.0 copy-start.3
  5.5 1.0 %copy-done.3 = bf16[64,4096]{1,0:T(8,128)(2,1)S(1)} copy-done((bf16[64,4096]{1,0:T(8,128)(2,1)S(1)}, bf16[64,4096]{1,0:T(8,128)(2,1)}, u32[]{:S(2)}) %copy-start.3) | copy-done | bytes 524312
  6.5 1.4 %moments.1 = (f32[16,256]{1,0:T(8,128)S(1)}, f32[512,128]{1,0:T(8,128)S(1)}) custom-call(s32[7]{0:T(128)S(1)} %stack.39.scal_ref, f32[256,2048]{1,0:T(8,128)S(1)} %bitcast.10, s32[1,512]{1,0:T(1,128)S(1)} %reshape.10.kind_ref, bf16[64,4096]{1,0:T(8,128)(2,1)S(1)} %copy-done.3), custom_call_target="tpu_custom_call" | custom-call | flops 2000000000 | bytes 1048576 | tf_op jit(solution)/shard_map/moments/pallas_call | solution.py:753
  7.9 1.5 %collective-permute-start = (f32[16,256]{1,0:T(8,128)S(1)}, f32[16,256]{1,0:T(8,128)S(1)}, u32[]{:S(2)}, u32[]{:S(2)}) collective-permute-start(f32[16,256]{1,0:T(8,128)S(1)} %get-tuple-element.23), channel_id=1, source_target_pairs={{0,1},{1,0},{2,3},{3,2},{4,5},{5,4},{6,7},{7,6},{8,9},{9,8},{10,11... | collective-permute-start | bytes 49160 | tf_op jit(solution)/shard_map/ppermute | solution.py:748
  9.4 3.3 %collective-permute-start.2 = (f32[40,2048]{1,0:T(8,128)S(1)}, f32[40,2048]{1,0:T(8,128)S(1)}, u32[]{:S(2)}, u32[]{:S(2)}) collective-permute-start(f32[40,2048]{1,0:T(8,128)S(1)} %get-tuple-element.28), channel_id=1, source_target_pairs={{0,2},{3,1},{2,4},{5,3},{4,6},{7,5},{6,8},{9,7},{8,10},{11,9},{10,... | collective-permute-start | bytes 983048 | tf_op jit(solution)/shard_map/ppermute | solution.py:757
  12.7 0.0 collective-permute-done
  12.8 2.3 %collective-permute-start.4 = (f32[16,128]{1,0:T(8,128)S(1)}, f32[16,128]{1,0:T(8,128)S(1)}, u32[]{:S(2)}, u32[]{:S(2)}) collective-permute-start(f32[16,128]{1,0:T(8,128)S(1)} %get-tuple-element.43), channel_id=1, source_target_pairs={{2,0},{4,2},{6,4},{8,6},{10,8},{12,10},{14,12},{16,14},{18,16},{20... | collective-permute-start | bytes 24584 | tf_op jit(solution)/shard_map/ppermute | solution.py:760
  15.0 2.0 %collective-permute-start.3 = (f32[16,128]{1,0:T(8,128)S(1)}, f32[16,128]{1,0:T(8,128)S(1)}, u32[]{:S(2)}, u32[]{:S(2)}) collective-permute-start(f32[16,128]{1,0:T(8,128)S(1)} %get-tuple-element.44), channel_id=1, source_target_pairs={{0,2},{2,4},{4,6},{6,8},{8,10},{10,12},{12,14},{14,16},{16,18},{18... | collective-permute-start | bytes 24584 | tf_op jit(solution)/shard_map/ppermute | solution.py:759
  17.1 0.0 copy-start.4
  17.1 2.9 %facesin.2 = (f32[256,2048]{1,0:T(8,128)S(1)}, f32[320,2048]{1,0:T(8,128)S(1)}, f32[320,64]{1,0:T(8,128)S(1)}) custom-call(s32[7]{0:T(128)S(1)} %stack.39.scal_ref, f32[256,2048]{1,0:T(8,128)S(1)} %bitcast.11, f32[16,256]{1,0:T(8,128)S(1)} %add.12.tot_ref, f32[512,128]{1,0:T(8,128)S(1)} %get-tuple-element.24.mask_ref, bf16[64,4096]{1,0:T(8,128)(2,1)S(1)} %copy-done.3), custom_call_target="tpu_custom_call" | custom-call | flops 6000000000 | bytes 1048576 | tf_op jit(solution)/shard_map/facesin/pallas_call | solution.py:761
  20.0 0.0 collective-permute-done.4.above_ref
  20.0 2.0 %collective-permute-done.3.below_ref = f32[16,128]{1,0:T(8,128)S(1)} collective-permute-done((f32[16,128]{1,0:T(8,128)S(1)}, f32[16,128]{1,0:T(8,128)S(1)}, u32[]{:S(2)}, u32[]{:S(2)}) %collective-permute-start.3) | collective-permute-done | bytes 8224 | tf_op jit(solution)/shard_map/ppermute | solution.py:759
  22.1 0.0 collective-permute-done.2.dn_ref
  22.1 0.0 collective-permute-done.1.upw_ref
  22.1 0.0 copy-done.4
  22.1 0.0 copy-start.2
  22.1 3.4 %faceb.2 = (f32[368,2048]{1,0:T(8,128)S(1)}, f32[16,768]{1,0:T(8,128)S(1)}) custom-call(s32[7]{0:T(128)S(1)} %stack.39.scal_ref, f32[256,2048]{1,0:T(8,128)S(1)} %get-tuple-element.25.cell_ref, f32[104,2048]{1,0:T(8,128)S(1)} %collective-permute-done.1.upw_ref, f32[40,2048]{1,0:T(8,128)S(1)} %collective-permute-done.2.dn_ref, ...), custom_call_target="tpu_custom_call" | custom-call | flops 6000000000 | bytes 1048576 | tf_op jit(solution)/shard_map/faceb/pallas_call | solution.py:762
  25.4 0.6 collective-permute-start.5
  26.1 3.5 %collective-permute-done.5.peer_ref = f32[16,768]{1,0:T(8,128)S(1)} collective-permute-done((f32[16,768]{1,0:T(8,128)S(1)}, f32[16,768]{1,0:T(8,128)S(1)}, u32[]{:S(2)}, u32[]{:S(2)}) %collective-permute-start.5) | collective-permute-done | bytes 49184 | tf_op jit(solution)/shard_map/ppermute | solution.py:748
  29.6 0.0 copy-done.2
  29.6 4.6 %renew.2 = (f32[256,2048]{1,0:T(8,128)S(1)}, f32[16,256]{1,0:T(8,128)S(1)}, f32[104,2048]{1,0:T(8,128)S(1)}, f32[40,2048]{1,0:T(8,128)S(1)}) custom-call(s32[7]{0:T(128)S(1)} %stack.39.scal_ref, f32[6]{0:T(128)S(1)} %copy-done.2, f32[256,2048]{1,0:T(8,128)S(1)} %bitcast.12, f32[256,2048]{1,0:T(8,128)S(1)} %get-tuple-element.25.cell_ref, ...), custom_call_target="tpu_custom_call" | custom-call | flops 6000000000 | bytes 1048576 | tf_op jit(solution)/shard_map/renew/pallas_call | solution.py:765
  34.2 1.9 %collective-permute-start.7 = (f32[104,2048]{1,0:T(8,128)S(1)}, f32[104,2048]{1,0:T(8,128)S(1)}, u32[]{:S(2)}, u32[]{:S(2)}) collective-permute-start(f32[104,2048]{1,0:T(8,128)S(1)} %get-tuple-element.36), channel_id=1, source_target_pairs={{2,0},{1,3},{4,2},{3,5},{6,4},{5,7},{8,6},{7,9},{10,8},{9,11},{12,... | collective-permute-start | bytes 2555912 | tf_op jit(solution)/shard_map/ppermute | solution.py:756
  36.1 1.0 %collective-permute-start.6 = (f32[16,256]{1,0:T(8,128)S(1)}, f32[16,256]{1,0:T(8,128)S(1)}, u32[]{:S(2)}, u32[]{:S(2)}) collective-permute-start(f32[16,256]{1,0:T(8,128)S(1)} %get-tuple-element.33), channel_id=1, source_target_pairs={{0,1},{1,0},{2,3},{3,2},{4,5},{5,4},{6,7},{7,6},{8,9},{9,8},{10,11... | collective-permute-start | bytes 49160 | tf_op jit(solution)/shard_map/ppermute | solution.py:748
  37.1 3.3 %collective-permute-start.8 = (f32[40,2048]{1,0:T(8,128)S(1)}, f32[40,2048]{1,0:T(8,128)S(1)}, u32[]{:S(2)}, u32[]{:S(2)}) collective-permute-start(f32[40,2048]{1,0:T(8,128)S(1)} %get-tuple-element.37), channel_id=1, source_target_pairs={{0,2},{3,1},{2,4},{5,3},{4,6},{7,5},{6,8},{9,7},{8,10},{11,9},{10,... | collective-permute-start | bytes 983048 | tf_op jit(solution)/shard_map/ppermute | solution.py:757
  40.3 0.0 collective-permute-done.6
  40.4 2.3 %collective-permute-start.10 = (f32[16,128]{1,0:T(8,128)S(1)}, f32[16,128]{1,0:T(8,128)S(1)}, u32[]{:S(2)}, u32[]{:S(2)}) collective-permute-start(f32[16,128]{1,0:T(8,128)S(1)} %get-tuple-element.41), channel_id=1, source_target_pairs={{2,0},{4,2},{6,4},{8,6},{10,8},{12,10},{14,12},{16,14},{18,16},{20... | collective-permute-start | bytes 24584 | tf_op jit(solution)/shard_map/ppermute | solution.py:760
  42.7 2.2 %collective-permute-start.9 = (f32[16,128]{1,0:T(8,128)S(1)}, f32[16,128]{1,0:T(8,128)S(1)}, u32[]{:S(2)}, u32[]{:S(2)}) collective-permute-start(f32[16,128]{1,0:T(8,128)S(1)} %get-tuple-element.42), channel_id=1, source_target_pairs={{0,2},{2,4},{4,6},{6,8},{8,10},{10,12},{12,14},{14,16},{16,18},{18... | collective-permute-start | bytes 24584 | tf_op jit(solution)/shard_map/ppermute | solution.py:759
  44.9 2.9 %facesin.3 = (f32[256,2048]{1,0:T(8,128)S(1)}, f32[320,2048]{1,0:T(8,128)S(1)}, f32[320,64]{1,0:T(8,128)S(1)}) custom-call(s32[7]{0:T(128)S(1)} %stack.39.scal_ref, f32[256,2048]{1,0:T(8,128)S(1)} %get-tuple-element.32.x_ref, f32[16,256]{1,0:T(8,128)S(1)} %add.13.tot_ref, f32[512,128]{1,0:T(8,128)S(1)} %get-tuple-element.24.mask_ref, ...), custom_call_target="tpu_custom_call" | custom-call | flops 6000000000 | bytes 1048576 | tf_op jit(solution)/shard_map/facesin/pallas_call | solution.py:761
  47.8 2.2 %collective-permute-done.10.above_ref = f32[16,128]{1,0:T(8,128)S(1)} collective-permute-done((f32[16,128]{1,0:T(8,128)S(1)}, f32[16,128]{1,0:T(8,128)S(1)}, u32[]{:S(2)}, u32[]{:S(2)}) %collective-permute-start.10) | collective-permute-done | bytes 8224 | tf_op jit(solution)/shard_map/ppermute | solution.py:760
  50.0 2.2 %collective-permute-done.9.below_ref = f32[16,128]{1,0:T(8,128)S(1)} collective-permute-done((f32[16,128]{1,0:T(8,128)S(1)}, f32[16,128]{1,0:T(8,128)S(1)}, u32[]{:S(2)}, u32[]{:S(2)}) %collective-permute-start.9) | collective-permute-done | bytes 8224 | tf_op jit(solution)/shard_map/ppermute | solution.py:759
  52.2 0.0 collective-permute-done.8.dn_ref
  52.2 0.0 collective-permute-done.7.upw_ref
  52.2 3.4 %faceb.3 = (f32[368,2048]{1,0:T(8,128)S(1)}, f32[16,768]{1,0:T(8,128)S(1)}) custom-call(s32[7]{0:T(128)S(1)} %stack.39.scal_ref, f32[256,2048]{1,0:T(8,128)S(1)} %get-tuple-element.34.cell_ref, f32[104,2048]{1,0:T(8,128)S(1)} %collective-permute-done.7.upw_ref, f32[40,2048]{1,0:T(8,128)S(1)} %collective-permute-done.8.dn_ref, ...), custom_call_target="tpu_custom_call" | custom-call | flops 6000000000 | bytes 1048576 | tf_op jit(solution)/shard_map/faceb/pallas_call | solution.py:762
  55.6 0.6 collective-permute-start.11
  56.2 3.5 %collective-permute-done.11.peer_ref = f32[16,768]{1,0:T(8,128)S(1)} collective-permute-done((f32[16,768]{1,0:T(8,128)S(1)}, f32[16,768]{1,0:T(8,128)S(1)}, u32[]{:S(2)}, u32[]{:S(2)}) %collective-permute-start.11) | collective-permute-done | bytes 49184 | tf_op jit(solution)/shard_map/ppermute | solution.py:748
  59.7 5.2 %renew.3 = f32[256,2048]{1,0:T(8,128)} custom-call(s32[7]{0:T(128)S(1)} %stack.39.scal_ref, f32[6]{0:T(128)S(1)} %copy-done.2, f32[256,2048]{1,0:T(8,128)S(1)} %get-tuple-element.32.x_ref, f32[256,2048]{1,0:T(8,128)S(1)} %get-tuple-element.34.cell_ref, f32[320,2048]{1,0:T(8,128)S(1)} %get-tuple-element.35.in_ref, ...), custom_call_target="tpu_custom_call" | custom-call | flops 6000000000 | bytes 1048576 | tf_op jit(solution)/shard_map/renew/pallas_call | solution.py:765
  (4 shorter events, 0.0 us)
Async XLA Ops:
  0.0 5.2 %copy-start.5 = (s32[64,8,8]{0,2,1:T(8,128)S(1)}, s32[64,8,8]{0,2,1:T(8,128)}, u32[]{:S(2)}) copy-start(s32[64,8,8]{0,2,1:T(8,128)} %param.5) | copy-start | bytes 49156
  0.1 1.6 %copy-start = (f32[4,8,8,2048]{3,2,1,0:T(8,128)S(1)}, f32[4,8,8,2048]{3,2,1,0:T(8,128)}, u32[]{:S(2)}) copy-start(f32[4,8,8,2048]{3,2,1,0:T(8,128)} %param.4) | copy-start | bytes 6291460
  1.7 3.8 %copy-start.1 = (f32[4,8,8,2048]{3,2,1,0:T(8,128)S(1)}, f32[4,8,8,2048]{3,2,1,0:T(8,128)}, u32[]{:S(2)}) copy-start(f32[4,8,8,2048]{3,2,1,0:T(8,128)} %param.4) | copy-start | bytes 6291460
  3.2 18.8 %collective-permute-start.1 = (f32[104,2048]{1,0:T(8,128)}, f32[104,2048]{1,0:T(8,128)S(1)}, u32[]{:S(2)}, u32[]{:S(2)}) collective-permute-start(f32[104,2048]{1,0:T(8,128)} %get-tuple-element.27), channel_id=1, source_target_pairs={{2,0},{1,3},{4,2},{3,5},{6,4},{5,7},{8,6},{7,9},{10,8},{9,11},{12,... | collective-permute-start | bytes 2555912 | tf_op jit(solution)/shard_map/ppermute | solution.py:756
  5.4 1.0 %copy-start.3 = (bf16[64,4096]{1,0:T(8,128)(2,1)S(1)}, bf16[64,4096]{1,0:T(8,128)(2,1)}, u32[]{:S(2)}) copy-start(bf16[64,4096]{1,0:T(8,128)(2,1)} %constant.26.clone.table_ref) | copy-start | bytes 1572868
  7.9 4.8 %collective-permute-start = (f32[16,256]{1,0:T(8,128)S(1)}, f32[16,256]{1,0:T(8,128)S(1)}, u32[]{:S(2)}, u32[]{:S(2)}) collective-permute-start(f32[16,256]{1,0:T(8,128)S(1)} %get-tuple-element.23), channel_id=1, source_target_pairs={{0,1},{1,0},{2,3},{3,2},{4,5},{5,4},{6,7},{7,6},{8,9},{9,8},{10,11... | collective-permute-start | bytes 49160 | tf_op jit(solution)/shard_map/ppermute | solution.py:748
  9.4 12.6 %collective-permute-start.2 = (f32[40,2048]{1,0:T(8,128)S(1)}, f32[40,2048]{1,0:T(8,128)S(1)}, u32[]{:S(2)}, u32[]{:S(2)}) collective-permute-start(f32[40,2048]{1,0:T(8,128)S(1)} %get-tuple-element.28), channel_id=1, source_target_pairs={{0,2},{3,1},{2,4},{5,3},{4,6},{7,5},{6,8},{9,7},{8,10},{11,9},{10,... | collective-permute-start | bytes 983048 | tf_op jit(solution)/shard_map/ppermute | solution.py:757
  12.8 7.3 %collective-permute-start.4 = (f32[16,128]{1,0:T(8,128)S(1)}, f32[16,128]{1,0:T(8,128)S(1)}, u32[]{:S(2)}, u32[]{:S(2)}) collective-permute-start(f32[16,128]{1,0:T(8,128)S(1)} %get-tuple-element.43), channel_id=1, source_target_pairs={{2,0},{4,2},{6,4},{8,6},{10,8},{12,10},{14,12},{16,14},{18,16},{20... | collective-permute-start | bytes 24584 | tf_op jit(solution)/shard_map/ppermute | solution.py:760
  15.0 7.0 %collective-permute-start.3 = (f32[16,128]{1,0:T(8,128)S(1)}, f32[16,128]{1,0:T(8,128)S(1)}, u32[]{:S(2)}, u32[]{:S(2)}) collective-permute-start(f32[16,128]{1,0:T(8,128)S(1)} %get-tuple-element.44), channel_id=1, source_target_pairs={{0,2},{2,4},{4,6},{6,8},{8,10},{10,12},{12,14},{14,16},{16,18},{18... | collective-permute-start | bytes 24584 | tf_op jit(solution)/shard_map/ppermute | solution.py:759
  17.1 5.0 %copy-start.4 = (bf16[64,4096]{1,0:T(8,128)(2,1)S(1)}, bf16[64,4096]{1,0:T(8,128)(2,1)}, u32[]{:S(2)}) copy-start(bf16[64,4096]{1,0:T(8,128)(2,1)} %constant.26.clone.table_ref) | copy-start | bytes 1572868
  22.1 7.5 %copy-start.2 = (f32[6]{0:T(128)S(1)}, f32[6]{0:T(128)}, u32[]{:S(2)}) copy-start(f32[6]{0:T(128)} %bound_ref.3) | copy-start | bytes 76
  25.4 4.1 %collective-permute-start.5 = (f32[16,768]{1,0:T(8,128)S(1)}, f32[16,768]{1,0:T(8,128)S(1)}, u32[]{:S(2)}, u32[]{:S(2)}) collective-permute-start(f32[16,768]{1,0:T(8,128)S(1)} %get-tuple-element.31.mom_ref), channel_id=1, source_target_pairs={{0,1},{1,0},{2,3},{3,2},{4,5},{5,4},{6,7},{7,6},{8,9},{9,8},{10,11... | collective-permute-start | bytes 147464 | tf_op jit(solution)/shard_map/ppermute | solution.py:748
  34.2 18.0 %collective-permute-start.7 = (f32[104,2048]{1,0:T(8,128)S(1)}, f32[104,2048]{1,0:T(8,128)S(1)}, u32[]{:S(2)}, u32[]{:S(2)}) collective-permute-start(f32[104,2048]{1,0:T(8,128)S(1)} %get-tuple-element.36), channel_id=1, source_target_pairs={{2,0},{1,3},{4,2},{3,5},{6,4},{5,7},{8,6},{7,9},{10,8},{9,11},{12,... | collective-permute-start | bytes 2555912 | tf_op jit(solution)/shard_map/ppermute | solution.py:756
  36.1 4.2 %collective-permute-start.6 = (f32[16,256]{1,0:T(8,128)S(1)}, f32[16,256]{1,0:T(8,128)S(1)}, u32[]{:S(2)}, u32[]{:S(2)}) collective-permute-start(f32[16,256]{1,0:T(8,128)S(1)} %get-tuple-element.33), channel_id=1, source_target_pairs={{0,1},{1,0},{2,3},{3,2},{4,5},{5,4},{6,7},{7,6},{8,9},{9,8},{10,11... | collective-permute-start | bytes 49160 | tf_op jit(solution)/shard_map/ppermute | solution.py:748
  37.1 15.1 %collective-permute-start.8 = (f32[40,2048]{1,0:T(8,128)S(1)}, f32[40,2048]{1,0:T(8,128)S(1)}, u32[]{:S(2)}, u32[]{:S(2)}) collective-permute-start(f32[40,2048]{1,0:T(8,128)S(1)} %get-tuple-element.37), channel_id=1, source_target_pairs={{0,2},{3,1},{2,4},{5,3},{4,6},{7,5},{6,8},{9,7},{8,10},{11,9},{10,... | collective-permute-start | bytes 983048 | tf_op jit(solution)/shard_map/ppermute | solution.py:757
  40.4 9.6 %collective-permute-start.10 = (f32[16,128]{1,0:T(8,128)S(1)}, f32[16,128]{1,0:T(8,128)S(1)}, u32[]{:S(2)}, u32[]{:S(2)}) collective-permute-start(f32[16,128]{1,0:T(8,128)S(1)} %get-tuple-element.41), channel_id=1, source_target_pairs={{2,0},{4,2},{6,4},{8,6},{10,8},{12,10},{14,12},{16,14},{18,16},{20... | collective-permute-start | bytes 24584 | tf_op jit(solution)/shard_map/ppermute | solution.py:760
  42.7 9.5 %collective-permute-start.9 = (f32[16,128]{1,0:T(8,128)S(1)}, f32[16,128]{1,0:T(8,128)S(1)}, u32[]{:S(2)}, u32[]{:S(2)}) collective-permute-start(f32[16,128]{1,0:T(8,128)S(1)} %get-tuple-element.42), channel_id=1, source_target_pairs={{0,2},{2,4},{4,6},{6,8},{8,10},{10,12},{12,14},{14,16},{16,18},{18... | collective-permute-start | bytes 24584 | tf_op jit(solution)/shard_map/ppermute | solution.py:759
  55.6 4.1 %collective-permute-start.11 = (f32[16,768]{1,0:T(8,128)S(1)}, f32[16,768]{1,0:T(8,128)S(1)}, u32[]{:S(2)}, u32[]{:S(2)}) collective-permute-start(f32[16,768]{1,0:T(8,128)S(1)} %get-tuple-element.40.mom_ref), channel_id=1, source_target_pairs={{0,1},{1,0},{2,3},{3,2},{4,5},{5,4},{6,7},{7,6},{8,9},{9,8},{10,11... | collective-permute-start | bytes 147464 | tf_op jit(solution)/shard_map/ppermute | solution.py:748
